TPU v7x, 128 devices: a whole 4x4x4 slice. The times are simulated.
128 devices in a mesh: book: 8 (over y, core), path: 16 (over z, x).
Axes of the slice: x: 4, y: 4, z: 4, core: 2. Of those that a mesh axis runs over, the one named last changes fastest.
Arguments:
- states: float32 [10, 20, 262144], P(None, None, ('book', 'path')), parts along dimension 2, may hold values from -7.5 to 7.5
- itm_flags: int32 [10, 262144], P(None, ('book', 'path')), parts along dimension 1, may hold values 0 or 1
- terminal: float32 [262144], P(('book', 'path')), parts along dimension 0, may hold values from -3.5 to 5.5
- strike: float32 [8], P('book'), parts along dimension 0, may hold values from 0.025 to 0.035
- date_index: int32 [262144], P(('book', 'path')), parts along dimension 0, may hold values from 0 to 9
Outputs:
- cash_flow: float32 [262144], P(('book', 'path')), parts along dimension 0
- book_price: float32 [8], P('book'), parts along dimension 0
- coefficients: float32 [80, 231], P('book'), parts along dimension 0
There are 8 independent parts, one for each index of `book`. A program takes and returns all parts, laid end to end along the dimension named above; each array names one. Nothing has to cross between parts.
All inputs are finite; a program needn't handle non-finite values. No bound on the sum of `itm_flags` on one device may be relied on, other than what follows from the above.
Results may differ from a plain program's by a relative error of at most 0.0003.
Values sent between devices are 32-bit elements; how exact they have to be, the bound alone decides.
A program may use at most 192 MiB of HBM per device.

v0:
```python
import jax
import jax.numpy as jnp
import numpy as np
from jax import lax
from jax.sharding import Mesh
from jax.sharding import PartitionSpec as P

PATH = ("path_0", "path_1")
BOOK_PATH = ("book", "path_0", "path_1")


ridge_weight = 0.05
temper_scale = 0.5
highest = lax.Precision.HIGHEST


def one_axis_at_a_time(shard, axes):
    for axis in axes:
        shard = lax.psum(shard, axis)
    return shard


def sent_to_all(shard, axis):
    length = lax.axis_size(axis)
    return lax.all_to_all(
        jnp.broadcast_to(shard[None], (length, *shard.shape)), axis, 0, 0, tiled=True
    )


def over_copies(shard, axis):
    return sent_to_all(shard, axis).sum(axis=0)


def swap_terms(factors, strike_level):
    forwards = 0.03 * jnp.exp(0.25 * factors)
    discount = jnp.cumprod(1.0 / (1.0 + 0.25 * forwards), axis=0)
    annuity = 0.25 * jnp.sum(discount, axis=0)
    swap_rate = (1.0 - discount[-1]) / annuity
    return (100.0 * annuity * (swap_rate - strike_level), discount[0])


def basis_of(scaled, pair_left, pair_right):
    ones_row = jnp.ones((1, scaled.shape[1]), jnp.float32)
    return jnp.concatenate([ones_row, scaled, scaled[pair_left] * scaled[pair_right]], axis=0)


def gram_only(basis_rows, money_flags):
    weighted = basis_rows * money_flags
    return lax.dot_general(
        weighted,
        basis_rows,
        (((1,), (1,)), ((), ())),
        precision=highest,
        preferred_element_type=jnp.float32,
    )


def system_of(gram_sums, path_count):
    return gram_sums / path_count + ridge_weight * jnp.eye(gram_sums.shape[0], dtype=jnp.float32)


def shards(states, itm_flags, terminal, strike, date_index):
    date_count, factor_count, local_paths = states.shape
    pair_left, pair_right = np.triu_indices(factor_count)
    total_paths = local_paths * lax.axis_size(PATH)
    value_now = terminal
    coef_list = []
    money_all = itm_flags.astype(jnp.float32)
    count_all, first_all, second_all = (
        one_axis_at_a_time(jnp.sum(money_all, axis=1), PATH),
        one_axis_at_a_time(jnp.sum(money_all[:, None, :] * states, axis=2), PATH),
        one_axis_at_a_time(jnp.sum(money_all[:, None, :] * states * states, axis=2), PATH),
    )
    mean_all = first_all / count_all[:, None]
    scale_all = jnp.sqrt(second_all / count_all[:, None] - mean_all * mean_all + 1e-05)
    local_list = []
    for date_step in range(date_count):
        scaled = (states[date_step] - mean_all[date_step][:, None]) / scale_all[date_step][:, None]
        local_list.append(gram_only(basis_of(scaled, pair_left, pair_right), money_all[date_step]))
    gram_stack = lax.psum(jnp.stack(local_list, axis=0), PATH)
    chol_list = [
        jnp.linalg.cholesky(system_of(gram_stack[date_step], count_all[date_step]))
        for date_step in range(date_count)
    ]
    for date_step in range(date_count - 1, -1, -1):
        factors = states[date_step]
        exercise, discount = swap_terms(factors, strike[0])
        value_now = value_now * discount
        money_flags = money_all[date_step]
        scaled = (factors - mean_all[date_step][:, None]) / scale_all[date_step][:, None]
        basis_rows = basis_of(scaled, pair_left, pair_right)
        rhs_local = jnp.dot(
            basis_rows * money_flags,
            value_now,
            precision=highest,
            preferred_element_type=jnp.float32,
        )
        rhs_total = over_copies(rhs_local, PATH)
        coef_vector = jax.scipy.linalg.cho_solve(
            (chol_list[date_step], True), rhs_total / count_all[date_step]
        )
        continuation = jnp.dot(
            coef_vector, basis_rows, precision=highest, preferred_element_type=jnp.float32
        )
        open_date = (date_index <= date_step).astype(jnp.float32)
        weights = jax.nn.sigmoid((exercise - continuation) / temper_scale) * money_flags * open_date
        value_now = value_now + weights * (exercise - value_now)
        coef_list.append(coef_vector)
    book_sum = one_axis_at_a_time(jnp.sum(value_now), PATH)
    book_price = jnp.reshape(book_sum / total_paths, (1,))
    return (value_now, book_price, jnp.stack(coef_list[::-1], axis=0))


def solution(mesh):
    split = Mesh(mesh.devices.reshape(mesh.shape["book"], 4, 4), ("book", "path_0", "path_1"))
    return jax.shard_map(
        shards,
        mesh=split,
        in_specs=(
            P(None, None, BOOK_PATH),
            P(None, BOOK_PATH),
            P(BOOK_PATH),
            P("book"),
            P(BOOK_PATH),
        ),
        out_specs=(P(BOOK_PATH), P("book"), P("book", None)),
        check_vma=False,
    )
```

profile of v0, /device:TPU:0, one launch (start us, length us, event | category | flops | bytes accessed | tf_op | source)
XLA Modules:
  0.0 1114.3 jit_solution(1723377565558352581)
XLA Ops:
  11.3 18.4 %all-reduce.4 = (f32[10,20]{1,0:T(8,128)S(1)}, f32[10]{0:T(128)S(1)}, f32[10,20]{1,0:T(8,128)S(1)}) all-reduce(f32[10,20]{1,0:T(8,128)S(1)} %get-tuple-element.80, f32[10]{0:T(128)S(1)} %convert_reduce_fusion, f32[10,20]{1,0:T(8,128)S(1)} %get-tuple-element.79), channel_id=1, replica_groups=mesh['book'=8,'path_0'=4,'path_1'=4] {'path_0'}, use_global_device_ids=true, to_apply=%region_9.0 | all-reduce | flops 410 | bytes 3280 | tf_op jit(solution)/shard_map/psum | solution.py:19
  29.7 17.0 %all-reduce.3 = (f32[10,20]{1,0:T(8,128)S(1)}, f32[10]{0:T(128)S(1)}, f32[10,20]{1,0:T(8,128)S(1)}) all-reduce(f32[10,20]{1,0:T(8,128)S(1)} %get-tuple-element.84, f32[10]{0:T(128)S(1)} %get-tuple-element.85, f32[10,20]{1,0:T(8,128)S(1)} %get-tuple-element.86), channel_id=1, replica_groups=mesh['book'=8,'path_0'=4,'path_1'=4] {'path_1'}, use_global_device_ids=true, to_apply=%region_10.11 | all-reduce | flops 410 | bytes 3280 | tf_op jit(solution)/shard_map/psum | solution.py:19
  184.8 69.2 %all-reduce.7.cloned.1.call-done = f32[10,231,231]{1,2,0:T(8,128)} async-done(((f32[10,231,231]{1,2,0:T(8,128)}), f32[10,231,231]{1,2,0:T(8,128)}) %all-reduce.7.cloned.1.call-update) | async-done | bytes 2134456 | tf_op jit(solution)/shard_map/psum | solution.py:80
  257.5 11.7 %cholesky.504 = f32[128,128]{1,0:T(8,128)S(1)} custom-call(f32[128,128]{1,0:T(8,128)S(1)} %cholesky.880), custom_call_target="Cholesky" | custom-call | tf_op jit(solution)/shard_map/jit(cholesky)/cholesky | solution.py:82
  269.9 9.8 custom-call.31
  304.6 12.1 %cholesky.846 = f32[128,128]{1,0:T(8,128)S(1)} custom-call(f32[128,128]{1,0:T(8,128)S(1)} %cholesky.907), custom_call_target="Cholesky" | custom-call | tf_op jit(solution)/shard_map/jit(cholesky)/cholesky | solution.py:82
  318.1 9.8 custom-call.49
  348.6 12.7 %cholesky.808 = f32[128,128]{1,0:T(8,128)S(1)} custom-call(f32[128,128]{1,0:T(8,128)} %cholesky.904), custom_call_target="Cholesky" | custom-call | tf_op jit(solution)/shard_map/jit(cholesky)/cholesky | solution.py:82
  363.2 10.6 custom-call.47
  377.2 10.2 cholesky.828
  396.5 12.5 %cholesky.770 = f32[128,128]{1,0:T(8,128)S(1)} custom-call(f32[128,128]{1,0:T(8,128)} %cholesky.901), custom_call_target="Cholesky" | custom-call | tf_op jit(solution)/shard_map/jit(cholesky)/cholesky | solution.py:82
  411.1 10.6 custom-call.45
  425.3 10.2 cholesky.790
  442.9 11.7 %cholesky.732 = f32[128,128]{1,0:T(8,128)S(1)} custom-call(f32[128,128]{1,0:T(8,128)S(1)} %cholesky.898), custom_call_target="Cholesky" | custom-call | tf_op jit(solution)/shard_map/jit(cholesky)/cholesky | solution.py:82
  484.1 11.7 %cholesky.694 = f32[128,128]{1,0:T(8,128)S(1)} custom-call(f32[128,128]{1,0:T(8,128)S(1)} %cholesky.895), custom_call_target="Cholesky" | custom-call | tf_op jit(solution)/shard_map/jit(cholesky)/cholesky | solution.py:82
  523.6 11.9 %cholesky.656 = f32[128,128]{1,0:T(8,128)S(1)} custom-call(f32[128,128]{1,0:T(8,128)S(1)} %cholesky.892), custom_call_target="Cholesky" | custom-call | tf_op jit(solution)/shard_map/jit(cholesky)/cholesky | solution.py:82
  536.9 9.8 custom-call.39
  561.8 11.7 %cholesky.618 = f32[128,128]{1,0:T(8,128)S(1)} custom-call(f32[128,128]{1,0:T(8,128)S(1)} %cholesky.889), custom_call_target="Cholesky" | custom-call | tf_op jit(solution)/shard_map/jit(cholesky)/cholesky | solution.py:82
  574.8 10.2 custom-call.37
  600.0 11.7 %cholesky.580 = f32[128,128]{1,0:T(8,128)S(1)} custom-call(f32[128,128]{1,0:T(8,128)S(1)} %cholesky.886), custom_call_target="Cholesky" | custom-call | tf_op jit(solution)/shard_map/jit(cholesky)/cholesky | solution.py:82
  613.1 9.8 custom-call.35
  638.1 11.7 %cholesky.542 = f32[128,128]{1,0:T(8,128)S(1)} custom-call(f32[128,128]{1,0:T(8,128)S(1)} %cholesky.883), custom_call_target="Cholesky" | custom-call | tf_op jit(solution)/shard_map/jit(cholesky)/cholesky | solution.py:82
  676.6 19.7 %custom-call.32 = f32[2,128,128]{1,2,0:T(8,128)S(1)} custom-call(f32[2,128,128]{2,1,0:T(8,128)S(1)} %pad_maximum_fusion.10), custom_call_target="InvertDiagBlocksLowerTriangular" | custom-call | tf_op jit(solution)/shard_map/jit(_cho_solve)/triangular_solve | solution.py:99
  719.7 21.1 %custom-call.50 = f32[2,128,128]{1,2,0:T(8,128)} custom-call(f32[2,128,128]{2,1,0:T(8,128)} %pad_maximum_fusion.19), custom_call_target="InvertDiagBlocksLowerTriangular" | custom-call | tf_op jit(solution)/shard_map/jit(_cho_solve)/triangular_solve | solution.py:99
  740.8 21.1 %custom-call.36 = f32[2,128,128]{1,2,0:T(8,128)} custom-call(f32[2,128,128]{2,1,0:T(8,128)} %pad_maximum_fusion.12), custom_call_target="InvertDiagBlocksLowerTriangular" | custom-call | tf_op jit(solution)/shard_map/jit(_cho_solve)/triangular_solve | solution.py:99
  761.9 21.1 %custom-call.38 = f32[2,128,128]{1,2,0:T(8,128)} custom-call(f32[2,128,128]{2,1,0:T(8,128)} %pad_maximum_fusion.13), custom_call_target="InvertDiagBlocksLowerTriangular" | custom-call | tf_op jit(solution)/shard_map/jit(_cho_solve)/triangular_solve | solution.py:99
  783.0 21.1 %custom-call.40 = f32[2,128,128]{1,2,0:T(8,128)} custom-call(f32[2,128,128]{2,1,0:T(8,128)} %pad_maximum_fusion.14), custom_call_target="InvertDiagBlocksLowerTriangular" | custom-call | tf_op jit(solution)/shard_map/jit(_cho_solve)/triangular_solve | solution.py:99
  804.1 21.1 %custom-call.42 = f32[2,128,128]{1,2,0:T(8,128)} custom-call(f32[2,128,128]{2,1,0:T(8,128)} %pad_maximum_fusion.15), custom_call_target="InvertDiagBlocksLowerTriangular" | custom-call | tf_op jit(solution)/shard_map/jit(_cho_solve)/triangular_solve | solution.py:99
  825.2 21.3 %custom-call.44 = f32[2,128,128]{1,2,0:T(8,128)} custom-call(f32[2,128,128]{2,1,0:T(8,128)} %pad_maximum_fusion.16), custom_call_target="InvertDiagBlocksLowerTriangular" | custom-call | tf_op jit(solution)/shard_map/jit(_cho_solve)/triangular_solve | solution.py:99
  846.5 21.1 %custom-call.46 = f32[2,128,128]{1,2,0:T(8,128)} custom-call(f32[2,128,128]{2,1,0:T(8,128)} %pad_maximum_fusion.17), custom_call_target="InvertDiagBlocksLowerTriangular" | custom-call | tf_op jit(solution)/shard_map/jit(_cho_solve)/triangular_solve | solution.py:99
  867.6 21.1 %custom-call.48 = f32[2,128,128]{1,2,0:T(8,128)} custom-call(f32[2,128,128]{2,1,0:T(8,128)} %pad_maximum_fusion.18), custom_call_target="InvertDiagBlocksLowerTriangular" | custom-call | tf_op jit(solution)/shard_map/jit(_cho_solve)/triangular_solve | solution.py:99
  888.7 21.1 %custom-call.34 = f32[2,128,128]{1,2,0:T(8,128)} custom-call(f32[2,128,128]{2,1,0:T(8,128)} %pad_maximum_fusion.11), custom_call_target="InvertDiagBlocksLowerTriangular" | custom-call | tf_op jit(solution)/shard_map/jit(_cho_solve)/triangular_solve | solution.py:99
  (684 shorter events, 557.4 us)
Async XLA Ops:
  7.2 39.6 %copy-start.142 = (s32[210]{0:T(256)S(1)}, s32[210]{0:T(256)}, u32[]{:S(2)}) copy-start(s32[210]{0:T(256)} %constant.243) | copy-start | bytes 2524
  7.2 39.6 %copy-start.143 = (s32[210]{0:T(256)S(1)}, s32[210]{0:T(256)}, u32[]{:S(2)}) copy-start(s32[210]{0:T(256)} %constant.242) | copy-start | bytes 2524
  9.2 117.4 %copy-start.71 = (f32[1,2048]{1,0:T(1,128)}, f32[1,2048]{1,0:T(1,128)S(1)}, u32[]{:S(2)}) copy-start(f32[1,2048]{1,0:T(1,128)S(1)} %get-tuple-element.145) | copy-start | bytes 24580
  9.2 126.6 %copy-start.75 = (f32[1,2048]{1,0:T(1,128)}, f32[1,2048]{1,0:T(1,128)S(1)}, u32[]{:S(2)}) copy-start(f32[1,2048]{1,0:T(1,128)S(1)} %get-tuple-element.144) | copy-start | bytes 24580
  9.2 129.3 %copy-start.77 = (f32[1,2048]{1,0:T(1,128)}, f32[1,2048]{1,0:T(1,128)S(1)}, u32[]{:S(2)}) copy-start(f32[1,2048]{1,0:T(1,128)S(1)} %get-tuple-element.143) | copy-start | bytes 24580
  9.2 132.0 %copy-start.79 = (f32[1,2048]{1,0:T(1,128)}, f32[1,2048]{1,0:T(1,128)S(1)}, u32[]{:S(2)}) copy-start(f32[1,2048]{1,0:T(1,128)S(1)} %get-tuple-element.142) | copy-start | bytes 24580
  9.3 134.7 %copy-start.81 = (f32[1,2048]{1,0:T(1,128)}, f32[1,2048]{1,0:T(1,128)S(1)}, u32[]{:S(2)}) copy-start(f32[1,2048]{1,0:T(1,128)S(1)} %get-tuple-element.141) | copy-start | bytes 24580
  9.3 137.6 %copy-start.83 = (f32[1,2048]{1,0:T(1,128)}, f32[1,2048]{1,0:T(1,128)S(1)}, u32[]{:S(2)}) copy-start(f32[1,2048]{1,0:T(1,128)S(1)} %get-tuple-element.140) | copy-start | bytes 24580
  9.3 140.3 %copy-start.85 = (f32[1,2048]{1,0:T(1,128)}, f32[1,2048]{1,0:T(1,128)S(1)}, u32[]{:S(2)}) copy-start(f32[1,2048]{1,0:T(1,128)S(1)} %get-tuple-element.139) | copy-start | bytes 24580
  9.3 143.0 %copy-start.88 = (f32[1,2048]{1,0:T(1,128)}, f32[1,2048]{1,0:T(1,128)S(1)}, u32[]{:S(2)}) copy-start(f32[1,2048]{1,0:T(1,128)S(1)} %get-tuple-element.138) | copy-start | bytes 24580
  9.3 145.7 %copy-start.90 = (f32[1,2048]{1,0:T(1,128)}, f32[1,2048]{1,0:T(1,128)S(1)}, u32[]{:S(2)}) copy-start(f32[1,2048]{1,0:T(1,128)S(1)} %get-tuple-element.137) | copy-start | bytes 24580
  9.3 148.4 %copy-start.96 = (f32[1,2048]{1,0:T(1,128)}, f32[1,2048]{1,0:T(1,128)S(1)}, u32[]{:S(2)}) copy-start(f32[1,2048]{1,0:T(1,128)S(1)} %get-tuple-element.146) | copy-start | bytes 24580
  60.6 97.1 %copy-start.127 = (f32[1,2048]{1,0:T(1,128)}, f32[1,2048]{1,0:T(1,128)S(1)}, u32[]{:S(2)}) copy-start(f32[1,2048]{1,0:T(1,128)S(1)} %broadcast.242) | copy-start | bytes 24580
  62.9 121.1 %all-to-all-start = ((f32[16,1,231]{2,1,0:T(1,128)}), f32[16,1,231]{2,1,0:T(1,128)S(1)}, u32[]{:S(2)}, u32[]{:S(2)}) async-start(f32[16,1,231]{2,1,0:T(1,128)} %broadcast_in_dim.208), calls=%async_computation | async-start | bytes 32768 | tf_op jit(solution)/shard_map/all_to_all | solution.py:25
  66.7 187.3 %all-reduce.7.cloned.1.call-start = ((), (), s32[]{:S(2)}) async-start(), calls=%async_computation.10 | async-start | bytes 4751360 | tf_op jit(solution)/shard_map/psum | solution.py:80
  634.2 42.3 %copy-start.52 = (f32[128,25]{1,0:T(8,128)S(1)}, f32[128,25]{1,0:T(8,128)}, u32[]{:S(2)}) copy-start(f32[128,25]{1,0:T(8,128)} %pad_convert_fusion) | copy-start | bytes 38404
  634.2 42.3 %copy-start.61 = (f32[103,103]{1,0:T(8,128)S(1)}, f32[103,103]{1,0:T(8,128)}, u32[]{:S(2)}) copy-start(f32[103,103]{1,0:T(8,128)} %triangular_solve.700) | copy-start | bytes 127312
  636.2 40.4 %copy-start.60 = (f32[1,128,128]{2,1,0:T(8,128)S(1)}, f32[1,128,128]{2,1,0:T(8,128)}, u32[]{:S(2)}) copy-start(f32[1,128,128]{2,1,0:T(8,128)} %slice_bitcast_fusion.19) | copy-start | bytes 196612
  637.9 61.2 %copy-start.128 = (f32[1,2048]{1,0:T(1,128)S(1)}, f32[1,2048]{1,0:T(1,128)}, u32[]{:S(2)}) copy-start(f32[1,2048]{1,0:T(1,128)} %copy-done.127) | copy-start | bytes 24580
  704.3 205.5 %all-to-all-start.1 = ((f32[16,1,231]{2,1,0:T(1,128)}), f32[16,1,231]{2,1,0:T(1,128)}, u32[]{:S(2)}, u32[]{:S(2)}) async-start(f32[16,1,231]{2,1,0:T(1,128)} %broadcast_in_dim.211), calls=%async_computation.1 | async-start | bytes 32768 | tf_op jit(solution)/shard_map/all_to_all | solution.py:25
  713.0 208.9 %copy-start.31 = (f32[210,2048]{1,0:T(8,128)S(1)}, f32[210,2048]{1,0:T(8,128)}, u32[]{:S(2)}) copy-start(f32[210,2048]{1,0:T(8,128)} %copy-done.30) | copy-start | bytes 5160964
  713.0 208.9 %copy-start.89 = (f32[1,2048]{1,0:T(1,128)S(1)}, f32[1,2048]{1,0:T(1,128)}, u32[]{:S(2)}) copy-start(f32[1,2048]{1,0:T(1,128)} %copy-done.88) | copy-start | bytes 24580
  924.3 14.9 %all-to-all-start.2 = ((f32[16,1,231]{2,1,0:T(1,128)}), f32[16,1,231]{2,1,0:T(1,128)S(1)}, u32[]{:S(2)}, u32[]{:S(2)}) async-start(f32[16,1,231]{2,1,0:T(1,128)} %broadcast_in_dim.214), calls=%async_computation.2 | async-start | bytes 32768 | tf_op jit(solution)/shard_map/all_to_all | solution.py:25
  951.0 11.0 all-to-all-start.3
  970.4 11.0 all-to-all-start.4
  990.0 11.4 %all-to-all-start.5 = ((f32[16,1,231]{2,1,0:T(1,128)}), f32[16,1,231]{2,1,0:T(1,128)S(1)}, u32[]{:S(2)}, u32[]{:S(2)}) async-start(f32[16,1,231]{2,1,0:T(1,128)} %broadcast_in_dim.223), calls=%async_computation.5 | async-start | bytes 32768 | tf_op jit(solution)/shard_map/all_to_all | solution.py:25
  1009.8 11.0 all-to-all-start.6
  1029.3 11.0 all-to-all-start.7
  1048.7 11.2 %all-to-all-start.8 = ((f32[16,1,231]{2,1,0:T(1,128)}), f32[16,1,231]{2,1,0:T(1,128)S(1)}, u32[]{:S(2)}, u32[]{:S(2)}) async-start(f32[16,1,231]{2,1,0:T(1,128)} %broadcast_in_dim.232), calls=%async_computation.8 | async-start | bytes 32768 | tf_op jit(solution)/shard_map/all_to_all | solution.py:25
  1067.7 37.1 %copy-start.136 = (f32[1,231]{1,0:T(1,128)S(1)}, f32[1,231]{1,0:T(1,128)}, u32[]{:S(2)}) copy-start(f32[1,231]{1,0:T(1,128)} %fusion.420) | copy-start | bytes 2776
  1067.8 37.1 %copy-start.137 = (f32[1,231]{1,0:T(1,128)S(1)}, f32[1,231]{1,0:T(1,128)}, u32[]{:S(2)}) copy-start(f32[1,231]{1,0:T(1,128)} %fusion.419) | copy-start | bytes 2776
  1068.4 11.0 all-to-all-start.9
  (123 other events, 1440.3 us)
Sparse Core Ops, SparseCore 0:
  160.6 93.2 all-reduce.6
where the time goes:
time: 1120 us; the launch traced here: 1110 us
  other arithmetic  630 us (56%)
  waiting for transfers between devices  127 us (11%)
  matrix products  123 us (11%)
  local copies, waits for them, and re-layouts  106 us (9%)
  blocking collectives  54.3 us (5%)
  starting transfers between devices  41.8 us (4%)
  between operations  31.9 us (3%)
    another operation x70, other arithmetic, shards(): jnp.linalg.cholesky(system_of(gram_stack[date_step], count_all[date_step]))  336 us
    another operation x34, other arithmetic, shards(): jax.scipy.linalg.cho_solve((chol_list[date_step], True), rhs_total / coun...  229 us
    psum x1, waiting for transfers between devices, shards(): gram_stack = lax.psum(jnp.stack(local_list, axis=0), PATH)  69.2 us
    all_to_all x10, waiting for transfers between devices, sent_to_all(): lax.all_to_all(jnp.broadcast_to(shard[None], (length, *shard.shape)), axi...  58 us
    psum x4, blocking collectives, one_axis_at_a_time(): shard = lax.psum(shard, axis)  54.3 us
    all_to_all x10, starting transfers between devices, sent_to_all(): lax.all_to_all(jnp.broadcast_to(shard[None], (length, *shard.shape)), axi...  41.5 us
    another operation x60, matrix products, shards(): jax.scipy.linalg.cho_solve((chol_list[date_step], True), rhs_total / coun...  33.7 us
    dot_general x10, matrix products, gram_only(): lax.dot_general(weighted, basis_rows, (((1,), (1,)), ((), ())), precision...  27.3 us
  transfers between devices with their start and end apart: 11, of which 9 were waited for; matrix products, arithmetic and copies ran while one was open for 27% of the time, Pallas kernels for 0%

commit v1 on v0

v1 whole, which is shorter than its diff:
```python
import functools

import jax
import jax.numpy as jnp
import numpy as np
from jax import lax
from jax.experimental import pallas as pl
from jax.experimental.pallas import tpu as pltpu
from jax.sharding import PartitionSpec as P

RIDGE = 0.05
TEMPER = 0.5
HIGHEST = lax.Precision.HIGHEST
f32 = jnp.float32
bf16 = jnp.bfloat16
GROUP = 16
DATES = 10
FACTORS = 20
BASIS = 231
ROWS = 232
PACKED = 264
OWNER = (1, 2, 3, 4, 6, 9, 11, 12, 13, 14)
MESH_ID = pl.DeviceIdType.MESH


def selectors():
    left, right = np.triu_indices(FACTORS)
    pairs = [(FACTORS, FACTORS)] + [(j, FACTORS) for j in range(FACTORS)]
    pairs += list(zip(left.tolist(), right.tolist()))
    sel = np.zeros((2, 256, 96), np.float32)
    for row, (a, b) in enumerate(pairs):
        for part in range(3):
            sel[0, row, 32 * part + a] = 1.0
            sel[1, row, 32 * part + b] = 1.0
    return jnp.asarray(sel, bf16)


def greet(me):
    barrier = pltpu.get_barrier_semaphore()
    for k in range(1, GROUP):
        pl.semaphore_signal(
            barrier, inc=1, device_id={"path": lax.rem(me + k, GROUP)}, device_id_type=MESH_ID
        )
    return barrier


def vmem():
    return pl.BlockSpec(memory_space=pltpu.VMEM)


def three_parts(a):
    one = a.astype(bf16)
    rest = a - one.astype(f32)
    two = rest.astype(bf16)
    three = (rest - two.astype(f32)).astype(bf16)
    return one, two, three


def stats_kernel(states, flags, mean_out, inv_out, count_out, part, slots, send_sem, recv_sem):
    me = lax.axis_index("path")
    barrier = greet(me)
    paths = states.shape[2]
    zero = jnp.zeros((24, 128), f32)
    for d in range(DATES):
        first = jnp.zeros((FACTORS, 128), f32)
        second = jnp.zeros((FACTORS, 128), f32)
        count = jnp.zeros((1, 128), f32)
        for c in range(paths // 128):
            z = states[d, :, 128 * c : 128 * c + 128]
            m = flags[d : d + 1, 128 * c : 128 * c + 128].astype(f32)
            mz = m * z
            first = first + mz
            second = second + mz * z
            count = count + m
        base = 64 * d
        part[base : base + 24, :] = zero
        part[base : base + FACTORS, :] = first
        part[base + 24 : base + 48, :] = zero
        part[base + 24 : base + 24 + FACTORS, :] = second
        part[base + 48 : base + 64, :] = jnp.zeros((16, 128), f32)
        part[base + 48 : base + 49, :] = count
    mine = [
        jnp.sum(part[128 * t : 128 * t + 128, :].T, axis=0, keepdims=True) for t in range(5)
    ]
    slots[me] = jnp.concatenate(mine + [jnp.zeros((3, 128), f32)], axis=0)
    pl.semaphore_wait(barrier, GROUP - 1)
    copies = []
    for k in range(1, GROUP):
        copies.append(
            pltpu.make_async_remote_copy(
                src_ref=slots.at[me],
                dst_ref=slots.at[me],
                send_sem=send_sem.at[k],
                recv_sem=recv_sem.at[k],
                device_id={"path": lax.rem(me + k, GROUP)},
                device_id_type=MESH_ID,
            )
        )
        copies[-1].start()
    for copy in copies:
        copy.wait_recv()
    total = slots[0]
    for k in range(1, GROUP):
        total = total + slots[k]
    columns = jnp.concatenate([total, jnp.zeros((120, 128), f32)], axis=0).T
    for d in range(DATES):
        base = 64 * (d % 2)
        column = jnp.broadcast_to(columns[base : base + 64, d // 2 : d // 2 + 1], (64, 128))
        count = jnp.broadcast_to(column[48:49, :], (24, 128))
        mean = column[0:24, :] / count
        variance = column[24:48, :] / count - mean * mean
        mean_out[d] = mean
        inv_out[d] = 1.0 / jnp.sqrt(variance + 1e-05)
        count_out[d] = count[0:8, :]
    for copy in copies:
        copy.wait_send()


def stats_call(states, flags):
    return pl.pallas_call(
        stats_kernel,
        name="stats",
        out_shape=(
            jax.ShapeDtypeStruct((DATES, 24, 128), f32),
            jax.ShapeDtypeStruct((DATES, 24, 128), f32),
            jax.ShapeDtypeStruct((DATES, 8, 128), f32),
        ),
        in_specs=[vmem()] * 2,
        out_specs=(vmem(),) * 3,
        scratch_shapes=[
            pltpu.VMEM((640, 128), f32),
            pltpu.VMEM((GROUP, 8, 128), f32),
            pltpu.SemaphoreType.DMA((GROUP,)),
            pltpu.SemaphoreType.DMA((GROUP,)),
        ],
        compiler_params=pltpu.CompilerParams(collective_id=0, has_side_effects=True),
    )(states, flags)


def fill_factors(y, states_d, mean, inv):
    paths = y.shape[1]
    for c in range(paths // 128):
        cut = slice(128 * c, 128 * c + 128)
        y[0:FACTORS, cut] = (states_d(cut) - mean[0:FACTORS]) * inv[0:FACTORS]


def fill_rest(y):
    paths = y.shape[1]
    y[FACTORS : FACTORS + 1, :] = jnp.ones((1, paths), f32)
    y[FACTORS + 1 : 32, :] = jnp.zeros((31 - FACTORS, paths), f32)


def basis_chunk(y_chunk, sel):
    stacked = jnp.concatenate(three_parts(y_chunk), axis=0)
    left = jnp.dot(sel[0], stacked, preferred_element_type=f32)
    right = jnp.dot(sel[1], stacked, preferred_element_type=f32)
    return left * right


def fill_basis(phi, y, sel, scale=None):
    paths = y.shape[1]
    width = min(256, paths)

    def step(i, carry):
        cut = pl.ds(pl.multiple_of(i * width, width), width)
        rows = basis_chunk(y[:, cut], sel)
        if scale is not None:
            rows = rows * scale(cut)
        phi[:, cut] = rows
        return carry

    lax.fori_loop(0, paths // width, step, 0)


def pack(full):
    rows = lax.broadcasted_iota(jnp.int32, (128, 128), 0)
    lanes = lax.broadcasted_iota(jnp.int32, (128, 128), 1)
    first = full[0:128, 0:128]
    mixed = jnp.where(rows > lanes, first, full[128:256, 128:256])
    diagonal = jnp.sum(jnp.where(rows == lanes, first, 0.0), axis=0, keepdims=True)
    return full[0:128, 128:256], mixed, jnp.broadcast_to(diagonal, (8, 128))


def unpack(cross, mixed, diagonal):
    rows = lax.broadcasted_iota(jnp.int32, (128, 128), 0)
    lanes = lax.broadcasted_iota(jnp.int32, (128, 128), 1)
    turned = mixed.T
    diagonal = jnp.broadcast_to(diagonal, (128, 128))
    first = jnp.where(rows > lanes, mixed, jnp.where(rows < lanes, turned, diagonal))
    last = jnp.where(rows <= lanes, mixed, turned)
    return first, cross, cross.T, last


def gram_kernel(states, flags, mean, inv, sel, out, y, phi):
    d = pl.program_id(0)

    @pl.when(d == 0)
    def _():
        fill_rest(y)

    fill_factors(y, lambda cut: states[0, :, cut], mean[0], inv[0])
    fill_basis(phi, y, sel, lambda cut: flags[pl.ds(d, 1), cut].astype(f32))
    rows = phi[...]
    full = lax.dot_general(
        rows, rows, (((1,), (1,)), ((), ())), precision=HIGHEST, preferred_element_type=f32
    )
    cross, mixed, diagonal = pack(full)
    out[0, 0:128, :] = cross
    out[0, 128:256, :] = mixed
    out[0, 256:264, :] = diagonal


def gram_call(states, flags, mean, inv, sel):
    paths = states.shape[2]
    return pl.pallas_call(
        gram_kernel,
        name="gram",
        grid=(DATES,),
        out_shape=jax.ShapeDtypeStruct((DATES, PACKED, 128), f32),
        in_specs=[
            pl.BlockSpec((1, FACTORS, paths), lambda d: (d, 0, 0)),
            pl.BlockSpec((DATES, paths), lambda d: (0, 0)),
            pl.BlockSpec((1, 24, 128), lambda d: (d, 0, 0)),
            pl.BlockSpec((1, 24, 128), lambda d: (d, 0, 0)),
            pl.BlockSpec((2, 256, 96), lambda d: (0, 0, 0)),
        ],
        out_specs=pl.BlockSpec((1, PACKED, 128), lambda d: (d, 0, 0)),
        scratch_shapes=[pltpu.VMEM((32, paths), f32), pltpu.VMEM((256, paths), f32)],
    )(states, flags, mean, inv, sel)


def collect_kernel(gram, out, slots, send_sem, recv_sem):
    me = lax.axis_index("path")
    barrier = greet(me)
    pl.semaphore_wait(barrier, GROUP - 1)

    def copy_of(d):
        offset = lax.rem(me - OWNER[d] + GROUP, GROUP)
        return pltpu.make_async_remote_copy(
            src_ref=gram.at[d],
            dst_ref=slots.at[offset],
            send_sem=send_sem.at[d],
            recv_sem=recv_sem.at[offset],
            device_id={"path": OWNER[d]},
            device_id_type=MESH_ID,
        )

    for d in range(DATES):

        @pl.when(me != OWNER[d])
        def _(d=d):
            copy_of(d).start()

    out[...] = jnp.zeros_like(out)
    for d in range(DATES):

        @pl.when(me == OWNER[d])
        def _(d=d):
            for k in range(1, GROUP):
                pltpu.make_async_remote_copy(
                    src_ref=gram.at[d],
                    dst_ref=slots.at[k],
                    send_sem=send_sem.at[d],
                    recv_sem=recv_sem.at[k],
                    device_id={"path": lax.rem(me + k, GROUP)},
                    device_id_type=MESH_ID,
                ).wait_recv()
            total = gram[d]
            for k in range(1, GROUP):
                total = total + slots[k]
            out[...] = total

    for d in range(DATES):

        @pl.when(me != OWNER[d])
        def _(d=d):
            copy_of(d).wait_send()


def collect_call(gram):
    return pl.pallas_call(
        collect_kernel,
        name="collect",
        out_shape=jax.ShapeDtypeStruct((PACKED, 128), f32),
        in_specs=[vmem()],
        out_specs=vmem(),
        scratch_shapes=[
            pltpu.VMEM((GROUP, PACKED, 128), f32),
            pltpu.SemaphoreType.DMA((DATES,)),
            pltpu.SemaphoreType.DMA((GROUP,)),
        ],
        compiler_params=pltpu.CompilerParams(collective_id=1, has_side_effects=True),
    )(gram)


def sweep_block(panel, b, start):
    height = panel.shape[0]
    columns = [
        jnp.broadcast_to(panel[:, start + c : start + c + 1], (height, 128)) for c in range(8)
    ]
    pivot = [column[8 * b : 8 * b + 8, :] for column in columns]
    row_of = lax.broadcasted_iota(jnp.int32, (8, 128), 0)
    for p in range(8):
        across = [jnp.broadcast_to(column[p : p + 1, :], (8, 128)) for column in pivot]
        inverse = 1.0 / across[p]
        own = pivot[p]
        here = row_of == p
        for c in range(8):
            if c == p:
                continue
            ratio = across[c] * inverse
            pivot[c] = jnp.where(here, ratio, pivot[c] - own * ratio)
        pivot[p] = jnp.where(here, -inverse, own * inverse)
    rows = panel[8 * b : 8 * b + 8, :]
    lane = lax.broadcasted_iota(jnp.int32, (8, 256), 1)
    swept = jnp.zeros((8, 256), f32)
    wide = [jnp.concatenate([column, column], axis=1) for column in pivot]
    for c in range(8):
        swept = swept - wide[c] * jnp.broadcast_to(rows[c : c + 1, :], (8, 256))
    for c in range(8):
        swept = jnp.where(lane == start + c, wide[c], swept)
    lane = lax.broadcasted_iota(jnp.int32, (height, 256), 1)
    rest = jnp.where((lane >= start) & (lane < start + 8), 0.0, panel)
    for c in range(8):
        wide_c = jnp.concatenate([columns[c], columns[c]], axis=1)
        rest = rest - wide_c * jnp.broadcast_to(swept[c : c + 1, :], (height, 256))
    pieces = [rest[8 * q : 8 * q + 8, :] for q in range(height // 8)]
    pieces[b] = swept
    return jnp.concatenate(pieces, axis=0)


def inverse_kernel(gram, count, out, work):
    scale = 1.0 / count[0:1, :]
    rows = lax.broadcasted_iota(jnp.int32, (128, 128), 0)
    lanes = lax.broadcasted_iota(jnp.int32, (128, 128), 1)
    ridge = jnp.where(rows == lanes, RIDGE, 0.0).astype(f32)
    first, cross, turned, last = unpack(
        gram[0:128, :] * scale, gram[128:256, :] * scale, gram[256:257, :] * scale
    )
    work[0:128, 0:128] = first + ridge
    work[0:128, 128:256] = cross
    work[128:256, 0:128] = turned
    work[128:256, 128:256] = last + ridge
    for top in range(0, ROWS, 32):
        before = work[top : top + 32, :]
        panel = before
        for b in range(4):
            if top + 8 * b < ROWS:
                panel = sweep_block(panel, b, top + 8 * b)
        if top + 32 > ROWS:
            keep = ROWS - top
            before = before[0:keep, :]
            panel = panel[0:keep, :]
        deep = before.shape[0]
        lane = lax.broadcasted_iota(jnp.int32, (256, 256), 1)
        change = lax.dot_general(
            before, panel, (((0,), (0,)), ((), ())), precision=HIGHEST, preferred_element_type=f32
        )
        work[...] = jnp.where((lane >= top) & (lane < top + deep), 0.0, work[...]) - change
        work[top : top + deep, :] = panel
    cross, mixed, diagonal = pack(-work[...])
    out[0:128, :] = cross
    out[128:256, :] = mixed
    out[256:264, :] = diagonal


def inverse_call(gram, count):
    return pl.pallas_call(
        inverse_kernel,
        name="inverse",
        out_shape=jax.ShapeDtypeStruct((PACKED, 128), f32),
        in_specs=[vmem()] * 2,
        out_specs=vmem(),
        scratch_shapes=[pltpu.VMEM((256, 256), f32)],
    )(gram, count)


def chain_kernel(
    states, flags, terminal, strike, date_index, mean, inv, count, sel, mine,
    cash_out, price_out, coef_out,
    y, phi, exercise, discount, value, packed, solve, slots, slots_price, coefs,
    bulk_send, bulk_recv, send_sem, recv_sem, price_send, price_recv,
):
    me = lax.axis_index("path")
    barrier = greet(me)
    paths = states.shape[2]
    chunks = paths // 128

    def prepare(d, par):
        mean_d = mean[d]
        inv_d = inv[d]
        for c in range(chunks):
            cut = slice(128 * c, 128 * c + 128)
            z = states[d, :, cut]
            y[0:FACTORS, cut] = (z - mean_d[0:FACTORS]) * inv_d[0:FACTORS]
            step = 1.0 / (1.0 + 0.25 * (0.03 * jnp.exp(0.25 * z)))
            running = step[0:1, :]
            discount[par, :, cut] = running
            total = running
            for j in range(1, FACTORS):
                running = running * step[j : j + 1, :]
                total = total + running
            annuity = 0.25 * total
            rate = (1.0 - running) / annuity
            exercise[par, :, cut] = 100.0 * annuity * (rate - strike[0])
        fill_basis(phi.at[par], y, sel)

    def bulk(d, k):
        return pltpu.make_async_remote_copy(
            src_ref=mine,
            dst_ref=packed.at[d],
            send_sem=bulk_send.at[k],
            recv_sem=bulk_recv.at[d],
            device_id={"path": lax.rem(me + k, GROUP)},
            device_id_type=MESH_ID,
        )

    def rhs_copy(par, k):
        return pltpu.make_async_remote_copy(
            src_ref=slots.at[par, me],
            dst_ref=slots.at[par, me],
            send_sem=send_sem.at[par, k],
            recv_sem=recv_sem.at[par, k],
            device_id={"path": lax.rem(me + k, GROUP)},
            device_id_type=MESH_ID,
        )

    def price_copy(k):
        return pltpu.make_async_remote_copy(
            src_ref=slots_price.at[me],
            dst_ref=slots_price.at[me],
            send_sem=price_send.at[k],
            recv_sem=price_recv.at[k],
            device_id={"path": lax.rem(me + k, GROUP)},
            device_id_type=MESH_ID,
        )

    fill_rest(y)
    pl.semaphore_wait(barrier, GROUP - 1)
    for d in range(DATES):

        @pl.when(me == OWNER[d])
        def _(d=d):
            for k in range(1, GROUP):
                bulk(d, k).start()
            packed[d] = mine[...]

    prepare(DATES - 1, 0)
    value[...] = terminal[...]
    coefs[...] = jnp.zeros_like(coefs)
    for d in range(DATES):

        @pl.when(me != OWNER[d])
        def _(d=d):
            bulk(d, 1).wait_recv()

    for d in range(DATES):

        @pl.when(me == OWNER[d])
        def _(d=d):
            for k in range(1, GROUP):
                bulk(d, k).wait_send()

    def date_step(t, carry):
        d = DATES - 1 - t
        par = lax.rem(t, 2)
        now = phi.at[par]
        held = value[...] * discount[par]
        money = flags[pl.ds(d, 1), :].astype(f32)
        weighted = money * held
        sums = jnp.zeros((ROWS, 128), f32)
        for c in range(chunks):
            cut = slice(128 * c, 128 * c + 128)
            sums = sums + now[0:ROWS, cut] * weighted[:, cut]
        low = jnp.sum(sums[0:128, :].T, axis=0, keepdims=True)
        high = jnp.concatenate([sums[128:ROWS, :], jnp.zeros((256 - ROWS, 128), f32)], axis=0)
        high = jnp.sum(high.T, axis=0, keepdims=True)
        slots[par, me] = jnp.concatenate([low, high], axis=0)
        for k in range(1, GROUP):
            rhs_copy(par, k).start()

        first, cross, turned, last = unpack(
            packed[d, 0:128, :], packed[d, 128:256, :], packed[d, 256:257, :]
        )
        solve[0:128, 0:128] = first
        solve[0:128, 128:256] = cross
        solve[128:256, 0:128] = turned
        solve[128:256, 128:256] = last
        prepare(jnp.maximum(d - 1, 0), 1 - par)

        for k in range(1, GROUP):
            rhs_copy(par, k).wait_recv()
        rhs = slots[par, 0]
        for k in range(1, GROUP):
            rhs = rhs + slots[par, k]
        rhs = rhs / count[d, 0:2, :]
        product = solve[0:ROWS, 0:128] * rhs[0:1, :] + solve[0:ROWS, 128:256] * rhs[1:2, :]
        coef = jnp.sum(product, axis=1, keepdims=True)
        coef = jnp.broadcast_to(coef, (ROWS, 128))
        lane = lax.broadcasted_iota(jnp.int32, (ROWS, 128), 1)
        coefs[0:ROWS, :] = jnp.where(lane == d, coef, coefs[0:ROWS, :])
        for c in range(chunks):
            cut = slice(128 * c, 128 * c + 128)
            continuation = jnp.sum(coef * now[0:ROWS, cut], axis=0, keepdims=True)
            gain = exercise[par, :, cut]
            open_date = (date_index[:, cut] <= d).astype(f32)
            weight = jax.nn.sigmoid((gain - continuation) / TEMPER) * money[:, cut] * open_date
            old = held[:, cut]
            value[:, cut] = old + weight * (gain - old)
        for k in range(1, GROUP):
            rhs_copy(par, k).wait_send()
        return carry

    lax.fori_loop(0, DATES, date_step, 0)

    total = jnp.zeros((1, 128), f32)
    for c in range(chunks):
        total = total + value[:, 128 * c : 128 * c + 128]
    slots_price[me] = total
    for k in range(1, GROUP):
        price_copy(k).start()
    cash_out[...] = value[...]
    turned = jnp.concatenate([coefs[0:128, :].T[0:16, :], coefs[128:256, :].T[0:16, :]], axis=1)
    coef_out[...] = turned[0:DATES, 0:BASIS]
    for k in range(1, GROUP):
        price_copy(k).wait_recv()
    total = slots_price[0]
    for k in range(1, GROUP):
        total = total + slots_price[k]
    price = jnp.sum(total, axis=1, keepdims=True) / (paths * GROUP)
    price_out[...] = jnp.broadcast_to(price, (1, 128))
    for k in range(1, GROUP):
        price_copy(k).wait_send()


def chain_call(states, flags, terminal, strike, date_index, mean, inv, count, sel, mine):
    paths = states.shape[2]
    return pl.pallas_call(
        chain_kernel,
        name="chain",
        out_shape=(
            jax.ShapeDtypeStruct((1, paths), f32),
            jax.ShapeDtypeStruct((1, 128), f32),
            jax.ShapeDtypeStruct((DATES, BASIS), f32),
        ),
        in_specs=[vmem()] * 3 + [pl.BlockSpec(memory_space=pltpu.SMEM)] + [vmem()] * 6,
        out_specs=(vmem(),) * 3,
        scratch_shapes=[
            pltpu.VMEM((32, paths), f32),
            pltpu.VMEM((2, 256, paths), f32),
            pltpu.VMEM((2, 1, paths), f32),
            pltpu.VMEM((2, 1, paths), f32),
            pltpu.VMEM((1, paths), f32),
            pltpu.VMEM((DATES, PACKED, 128), f32),
            pltpu.VMEM((256, 256), f32),
            pltpu.VMEM((2, GROUP, 2, 128), f32),
            pltpu.VMEM((GROUP, 1, 128), f32),
            pltpu.VMEM((256, 128), f32),
            pltpu.SemaphoreType.DMA((GROUP,)),
            pltpu.SemaphoreType.DMA((DATES,)),
            pltpu.SemaphoreType.DMA((2, GROUP)),
            pltpu.SemaphoreType.DMA((2, GROUP)),
            pltpu.SemaphoreType.DMA((GROUP,)),
            pltpu.SemaphoreType.DMA((GROUP,)),
        ],
        compiler_params=pltpu.CompilerParams(collective_id=2, has_side_effects=True),
    )(states, flags, terminal, strike, date_index, mean, inv, count, sel, mine)


def shards(states, flags, terminal, strike, date_index):
    paths = states.shape[2]
    sel = selectors()
    mean, inv, count = stats_call(states, flags)
    gram = gram_call(states, flags, mean, inv, sel)
    mine = collect_call(gram)
    me = lax.axis_index("path")
    own_count = count[0]
    for d in range(1, DATES):
        own_count = jnp.where(me == OWNER[d], count[d], own_count)
    packed = inverse_call(mine, own_count)
    cash, price, coefs = chain_call(
        states, flags, terminal.reshape(1, paths), strike, date_index.reshape(1, paths),
        mean, inv, count, sel, packed,
    )
    return cash.reshape(paths), price[0, 0:1], coefs


def solution(mesh):
    both = ("book", "path")
    return jax.shard_map(
        shards,
        mesh=mesh,
        in_specs=(P(None, None, both), P(None, both), P(both), P("book"), P(both)),
        out_specs=(P(both), P("book"), P("book", None)),
        check_vma=False,
    )
```

time: 1120 us -> 200 us (0.18)
  other arithmetic: 630 us -> 0.6 us
  Pallas kernels: 0 us -> 194 us
  waiting for transfers between devices: 127 us -> 0 us
  matrix products: 123 us -> 0 us
  local copies, waits for them, and re-layouts: 106 us -> 2.62 us
  blocking collectives: 54.3 us -> 0 us
  starting transfers between devices: 41.8 us -> 0 us
  between operations: 31.9 us -> 3.03 us
    another operation x124 -> x0, other arithmetic: 573 us -> none  [the longest x70 336 us: shards(): jnp.linalg.cholesky(system_of(gram_stack[date_step], count_all[date_step]))]
    pallas_call x0 -> x5, Pallas kernels: none -> 194 us  [the longest x1 100 us: chain_call(): pl.pallas_call(chain_kernel, name='chain', out_shape=(jax.ShapeDtypeStruc...]
    psum x1 -> x0, waiting for transfers between devices: 69.2 us -> none  [shards(): gram_stack = lax.psum(jnp.stack(local_list, axis=0), PATH)]
    dot_general x30 -> x0, matrix products: 69.1 us -> none  [the longest x10 27.3 us: gram_only(): lax.dot_general(weighted, basis_rows, (((1,), (1,)), ((), ())), precision...]
    all_to_all x10 -> x0, waiting for transfers between devices: 58 us -> none  [sent_to_all(): lax.all_to_all(jnp.broadcast_to(shard[None], (length, *shard.shape)), axi...]
    psum x4 -> x0, blocking collectives: 54.3 us -> none  [one_axis_at_a_time(): shard = lax.psum(shard, axis)]
    another operation x80 -> x0, matrix products: 53.7 us -> none  [the longest x60 33.7 us: shards(): jax.scipy.linalg.cho_solve((chol_list[date_step], True), rhs_total / coun...]
    gather x20 -> x0, local copies, waits for them, and re-layouts: 49.5 us -> none  [the longest x10 25.1 us: basis_of(): scaled[pair_right]]
  transfers between devices with their start and end apart: 11 -> 0, of which waited for: 9 -> 0; matrix products, arithmetic and copies ran while one was open for 27% -> 0% of each run, Pallas kernels for 0% -> 0%
where the time goes in v1:
time: 200 us
  Pallas kernels  194 us (97%)
  between operations  3.03 us (2%)
  local copies, waits for them, and re-layouts  2.62 us (1%)
    pallas_call x1, Pallas kernels, chain_call(): pl.pallas_call(chain_kernel, name='chain', out_shape=(jax.ShapeDtypeStruc...  100 us
    pallas_call x1, Pallas kernels, gram_call(): pl.pallas_call(gram_kernel, name='gram', grid=(DATES,), out_shape=jax.Sha...  38.1 us
    pallas_call x1, Pallas kernels, collect_call(): pl.pallas_call(collect_kernel, name='collect', out_shape=jax.ShapeDtypeSt...  28.9 us
    pallas_call x1, Pallas kernels, stats_call(): pl.pallas_call(stats_kernel, name='stats', out_shape=(jax.ShapeDtypeStruc...  13.4 us
    pallas_call x1, Pallas kernels, inverse_call(): pl.pallas_call(inverse_kernel, name='inverse', out_shape=jax.ShapeDtypeSt...  12.8 us

profile of v1, /device:TPU:0, one launch (start us, length us, event | category | flops | bytes accessed | tf_op | source)
XLA Modules:
  0.0 200.1 jit_solution(714571703743663751)
XLA Ops:
  1.3 13.4 %stats.1 = (f32[10,24,128]{2,1,0:T(8,128)}, f32[10,24,128]{2,1,0:T(8,128)}, f32[10,8,128]{2,1,0:T(8,128)}) custom-call(f32[10,20,2048]{2,1,0:T(8,128)} %states.5, s32[10,2048]{1,0:T(8,128)} %flags.5), custom_call_target="tpu_custom_call" | custom-call | tf_op jit(solution)/shard_map/stats/pallas_call | solution.py:120
  14.7 0.0 copy-start
  14.7 38.1 %gram.1 = f32[10,264,128]{2,1,0:T(8,128)} custom-call(f32[10,20,2048]{2,1,0:T(8,128)} %states.5, s32[10,2048]{1,0:T(8,128)} %flags.5, f32[10,24,128]{2,1,0:T(8,128)} %get-tuple-element.9.mean, f32[10,24,128]{2,1,0:T(8,128)} %get-tuple-element.10.inv, bf16[2,256,96]{2,1,0:T(8,128)(2,1)} %constant.24.clone.sel), custom_call_target="tpu_custom_call" | custom-call | tf_op jit(solution)/shard_map/gram/pallas_call | solution.py:215
  52.8 28.9 %collect.1.gram = f32[264,128]{1,0:T(8,128)} custom-call(f32[10,264,128]{2,1,0:T(8,128)} %gram.1), custom_call_target="tpu_custom_call" | custom-call | tf_op jit(solution)/shard_map/collect/pallas_call | solution.py:281
  81.8 0.0 copy-done
  81.8 0.6 select_bitcast_fusion.count
  82.4 12.8 %inverse.1.mine = f32[264,128]{1,0:T(8,128)} custom-call(f32[264,128]{1,0:T(8,128)} %collect.1.gram, f32[8,128]{1,0:T(8,128)} %select_bitcast_fusion.count), custom_call_target="tpu_custom_call" | custom-call | tf_op jit(solution)/shard_map/inverse/pallas_call | solution.py:368
  95.3 100.5 %chain.1 = (f32[1,2048]{1,0:T(1,128)}, f32[1,128]{1,0:T(1,128)}, f32[10,231]{1,0:T(8,128)}) custom-call(f32[10,20,2048]{2,1,0:T(8,128)} %states.5, s32[10,2048]{1,0:T(8,128)} %flags.5, f32[1,2048]{1,0:T(1,128)} %bitcast.7, f32[1]{0:T(128)S(6)} %copy.12.strike, s32[1,2048]{1,0:T(1,128)} %bitcast.8, f32[10,24,128]{2,1,0:T(8,128)} %get-tuple-element.9.mean, ...), custom_call_target="tpu_custom_call" | custom-call | tf_op jit(solution)/shard_map/chain/pallas_call | solution.py:538
  195.7 1.3 copy.13
  197.6 1.3 copy.15
Async XLA Ops:
  14.7 67.1 %copy-start = (f32[10,8,128]{2,1,0:T(8,128)S(1)}, f32[10,8,128]{2,1,0:T(8,128)}, u32[]{:S(2)}) copy-start(f32[10,8,128]{2,1,0:T(8,128)} %get-tuple-element.11.count) | copy-start | bytes 122884

commit v2 on v1

--- a/solution.py
+++ b/solution.py
@@ -19,7 +19,9 @@
 BASIS = 231
 ROWS = 232
 PACKED = 264
-OWNER = (1, 2, 3, 4, 6, 9, 11, 12, 13, 14)
+HALF = 136
+SIDE = 4
+LAG = 2
 MESH_ID = pl.DeviceIdType.MESH
 
 
@@ -35,6 +37,14 @@
     return jnp.asarray(sel, bf16)
 
 
+def owner_x(d):
+    return d % SIDE
+
+
+def owner_z(d):
+    return (d % SIDE + d // SIDE) % SIDE
+
+
 def greet(me):
     barrier = pltpu.get_barrier_semaphore()
     for k in range(1, GROUP):
@@ -56,7 +66,76 @@
     return one, two, three
 
 
-def stats_kernel(states, flags, mean_out, inv_out, count_out, part, slots, send_sem, recv_sem):
+def fill_factors(y, states_d, mean, inv):
+    paths = y.shape[1]
+    for c in range(paths // 128):
+        cut = slice(128 * c, 128 * c + 128)
+        y[0:FACTORS, cut] = (states_d(cut) - mean[0:FACTORS]) * inv[0:FACTORS]
+
+
+def fill_rest(y):
+    paths = y.shape[1]
+    y[FACTORS : FACTORS + 1, :] = jnp.ones((1, paths), f32)
+    y[FACTORS + 1 : 32, :] = jnp.zeros((31 - FACTORS, paths), f32)
+
+
+def basis_chunk(y_chunk, sel):
+    stacked = jnp.concatenate(three_parts(y_chunk), axis=0)
+    left = jnp.dot(sel[0], stacked, preferred_element_type=f32)
+    right = jnp.dot(sel[1], stacked, preferred_element_type=f32)
+    return left * right
+
+
+def over_chunks(paths, body):
+    width = min(256, paths)
+
+    def step(i, carry):
+        body(pl.ds(pl.multiple_of(i * width, width), width))
+        return carry
+
+    lax.fori_loop(0, paths // width, step, 0)
+
+
+def fill_basis(phi, y, sel):
+    def body(cut):
+        phi[:, cut] = basis_chunk(y[:, cut], sel)
+
+    over_chunks(y.shape[1], body)
+
+
+def triangle():
+    rows = lax.broadcasted_iota(jnp.int32, (128, 128), 0)
+    lanes = lax.broadcasted_iota(jnp.int32, (128, 128), 1)
+    return rows, lanes
+
+
+def pack(first, last):
+    rows, lanes = triangle()
+    mixed = jnp.where(rows > lanes, first, last)
+    diagonal = jnp.sum(jnp.where(rows == lanes, first, 0.0), axis=0, keepdims=True)
+    return mixed, jnp.broadcast_to(diagonal, (8, 128))
+
+
+def unpack(cross, mixed, diagonal):
+    rows, lanes = triangle()
+    turned = mixed.T
+    diagonal = jnp.broadcast_to(diagonal, (128, 128))
+    first = jnp.where(rows > lanes, mixed, jnp.where(rows < lanes, turned, diagonal))
+    last = jnp.where(rows <= lanes, mixed, turned)
+    return first, cross, cross.T, last
+
+
+def wait_all(copies):
+    for copy in copies:
+        copy.wait_recv()
+
+
+def front_kernel(
+    states, flags, sel, mean_out, inv_out, count_out, system_out,
+    part, slots, y, parts, gram, slot_a, slot_b, sum_a, sum_b, last_a, last_b,
+    send_sem, recv_sem, send_a, send_b, recv_a, recv_b,
+    send_last_a, send_last_b, recv_last_a, recv_last_b,
+):
     me = lax.axis_index("path")
     barrier = greet(me)
     paths = states.shape[2]
@@ -97,8 +176,8 @@
             )
         )
         copies[-1].start()
-    for copy in copies:
-        copy.wait_recv()
+    fill_rest(y)
+    wait_all(copies)
     total = slots[0]
     for k in range(1, GROUP):
         total = total + slots[k]
@@ -112,185 +191,206 @@
         mean_out[d] = mean
         inv_out[d] = 1.0 / jnp.sqrt(variance + 1e-05)
         count_out[d] = count[0:8, :]
+
+    my_z, my_x = me // SIDE, lax.rem(me, SIDE)
+
+    def copy_a(d, k):
+        return pltpu.make_async_remote_copy(
+            src_ref=gram.at[d, 0:HALF],
+            dst_ref=slot_a.at[d // SIDE, k],
+            send_sem=send_a.at[d],
+            recv_sem=recv_a.at[d // SIDE, k],
+            device_id={"path": my_z * SIDE + owner_x(d)},
+            device_id_type=MESH_ID,
+        )
+
+    def copy_b(d, k):
+        return pltpu.make_async_remote_copy(
+            src_ref=gram.at[d, HALF:PACKED],
+            dst_ref=slot_b.at[d // SIDE, k],
+            send_sem=send_b.at[d],
+            recv_sem=recv_b.at[d // SIDE, k],
+            device_id={"path": owner_z(d) * SIDE + my_x},
+            device_id_type=MESH_ID,
+        )
+
+    def last_copy_a(d, k):
+        return pltpu.make_async_remote_copy(
+            src_ref=sum_a.at[d // SIDE],
+            dst_ref=last_a.at[k],
+            send_sem=send_last_a.at[d // SIDE],
+            recv_sem=recv_last_a.at[k],
+            device_id={"path": owner_z(d) * SIDE + my_x},
+            device_id_type=MESH_ID,
+        )
+
+    def last_copy_b(d, k):
+        return pltpu.make_async_remote_copy(
+            src_ref=sum_b.at[d // SIDE],
+            dst_ref=last_b.at[k],
+            send_sem=send_last_b.at[d // SIDE],
+            recv_sem=recv_last_b.at[k],
+            device_id={"path": my_z * SIDE + owner_x(d)},
+            device_id_type=MESH_ID,
+        )
+
+    def compute(d):
+        fill_factors(y, lambda cut: states[d, :, cut], mean_out[d], inv_out[d])
+
+        def body(cut):
+            rows = basis_chunk(y[:, cut], sel) * flags[pl.ds(d, 1), cut].astype(f32)
+            one, two, three = three_parts(rows)
+            parts[0:256, cut] = one
+            parts[256:512, cut] = two
+            parts[512:768, cut] = three
+
+        over_chunks(paths, body)
+        lanes = (((1,), (1,)), ((), ()))
+        wide = lax.dot_general(parts[0:256, :], parts[...], lanes, preferred_element_type=f32)
+        small = lax.dot_general(
+            parts[256:512, :], parts[256:512, :], lanes, preferred_element_type=f32
+        )
+        main = wide[:, 0:256] + small
+        side = wide[:, 256:512] + wide[:, 512:768]
+        low, high = slice(0, 128), slice(128, 256)
+        gram[d, 0:128, :] = main[low, high] + (side[low, high] + side[high, low].T)
+        mixed, diagonal = pack(
+            main[low, low] + (side[low, low] + side[low, low].T),
+            main[high, high] + (side[high, high] + side[high, high].T),
+        )
+        gram[d, 128:256, :] = mixed
+        gram[d, 256:264, :] = diagonal
+
+    def send(d):
+        k_x = lax.rem(my_x - owner_x(d) + SIDE, SIDE)
+        k_z = lax.rem(my_z - owner_z(d) + SIDE, SIDE)
+
+        @pl.when(k_x != 0)
+        def _():
+            copy_a(d, k_x).start()
+
+        @pl.when(k_z != 0)
+        def _():
+            copy_b(d, k_z).start()
+
+    def collect(d):
+        q = d // SIDE
+        k_x = lax.rem(my_x - owner_x(d) + SIDE, SIDE)
+        k_z = lax.rem(my_z - owner_z(d) + SIDE, SIDE)
+
+        @pl.when(k_x == 0)
+        def _():
+            for k in range(1, SIDE):
+                copy_a(d, k).wait_recv()
+            sum_a[q] = (gram[d, 0:HALF] + slot_a[q, 1]) + (slot_a[q, 2] + slot_a[q, 3])
+
+            @pl.when(k_z != 0)
+            def _():
+                last_copy_a(d, k_z).start()
+
+        @pl.when(k_z == 0)
+        def _():
+            for k in range(1, SIDE):
+                copy_b(d, k).wait_recv()
+            sum_b[q] = (gram[d, HALF:PACKED] + slot_b[q, 1]) + (slot_b[q, 2] + slot_b[q, 3])
+
+            @pl.when(k_x != 0)
+            def _():
+                last_copy_b(d, k_x).start()
+
+    def date_step(d, carry):
+        compute(d)
+        send(d)
+
+        @pl.when(d >= LAG)
+        def _():
+            collect(d - LAG)
+
+        return carry
+
+    lax.fori_loop(0, DATES, date_step, 0)
+    lax.fori_loop(DATES - LAG, DATES, lambda d, carry: (collect(d), carry)[1], 0)
+
+    own_q = lax.rem(my_z - my_x + SIDE, SIDE)
+    own = own_q * SIDE + my_x
+    system_out[...] = jnp.zeros_like(system_out)
+
+    @pl.when(own < DATES)
+    def _():
+        for k in range(1, SIDE):
+            last_copy_a(own, k).wait_recv()
+            last_copy_b(own, k).wait_recv()
+        scale = 1.0 / count_out[own, 0:1, :]
+        system_out[0:HALF] = ((sum_a[own_q] + last_a[1]) + (last_a[2] + last_a[3])) * scale
+        system_out[HALF:PACKED] = ((sum_b[own_q] + last_b[1]) + (last_b[2] + last_b[3])) * scale
+
+    def finish(d, carry):
+        k_x = lax.rem(my_x - owner_x(d) + SIDE, SIDE)
+        k_z = lax.rem(my_z - owner_z(d) + SIDE, SIDE)
+
+        @pl.when(k_x != 0)
+        def _():
+            copy_a(d, k_x).wait_send()
+
+        @pl.when(k_z != 0)
+        def _():
+            copy_b(d, k_z).wait_send()
+
+        @pl.when((k_x == 0) & (k_z != 0))
+        def _():
+            last_copy_a(d, k_z).wait_send()
+
+        @pl.when((k_z == 0) & (k_x != 0))
+        def _():
+            last_copy_b(d, k_x).wait_send()
+
+        return carry
+
+    lax.fori_loop(0, DATES, finish, 0)
     for copy in copies:
         copy.wait_send()
 
 
-def stats_call(states, flags):
+def front_call(states, flags, sel):
+    paths = states.shape[2]
+    columns = DATES // SIDE + 1
+    dma = pltpu.SemaphoreType.DMA
     return pl.pallas_call(
-        stats_kernel,
-        name="stats",
+        front_kernel,
+        name="front",
         out_shape=(
             jax.ShapeDtypeStruct((DATES, 24, 128), f32),
             jax.ShapeDtypeStruct((DATES, 24, 128), f32),
             jax.ShapeDtypeStruct((DATES, 8, 128), f32),
+            jax.ShapeDtypeStruct((PACKED, 128), f32),
         ),
-        in_specs=[vmem()] * 2,
-        out_specs=(vmem(),) * 3,
+        in_specs=[vmem()] * 3,
+        out_specs=(vmem(),) * 4,
         scratch_shapes=[
             pltpu.VMEM((640, 128), f32),
             pltpu.VMEM((GROUP, 8, 128), f32),
-            pltpu.SemaphoreType.DMA((GROUP,)),
-            pltpu.SemaphoreType.DMA((GROUP,)),
+            pltpu.VMEM((32, paths), f32),
+            pltpu.VMEM((768, paths), bf16),
+            pltpu.VMEM((DATES, PACKED, 128), f32),
+            pltpu.VMEM((columns, SIDE, HALF, 128), f32),
+            pltpu.VMEM((columns, SIDE, PACKED - HALF, 128), f32),
+            pltpu.VMEM((columns, HALF, 128), f32),
+            pltpu.VMEM((columns, PACKED - HALF, 128), f32),
+            pltpu.VMEM((SIDE, HALF, 128), f32),
+            pltpu.VMEM((SIDE, PACKED - HALF, 128), f32),
+            dma((GROUP,)),
+            dma((GROUP,)),
+            dma((DATES,)),
+            dma((DATES,)),
+            dma((columns, SIDE)),
+            dma((columns, SIDE)),
+            dma((columns,)),
+            dma((columns,)),
+            dma((SIDE,)),
+            dma((SIDE,)),
         ],
         compiler_params=pltpu.CompilerParams(collective_id=0, has_side_effects=True),
-    )(states, flags)
-
-
-def fill_factors(y, states_d, mean, inv):
-    paths = y.shape[1]
-    for c in range(paths // 128):
-        cut = slice(128 * c, 128 * c + 128)
-        y[0:FACTORS, cut] = (states_d(cut) - mean[0:FACTORS]) * inv[0:FACTORS]
-
-
-def fill_rest(y):
-    paths = y.shape[1]
-    y[FACTORS : FACTORS + 1, :] = jnp.ones((1, paths), f32)
-    y[FACTORS + 1 : 32, :] = jnp.zeros((31 - FACTORS, paths), f32)
-
-
-def basis_chunk(y_chunk, sel):
-    stacked = jnp.concatenate(three_parts(y_chunk), axis=0)
-    left = jnp.dot(sel[0], stacked, preferred_element_type=f32)
-    right = jnp.dot(sel[1], stacked, preferred_element_type=f32)
-    return left * right
-
-
-def fill_basis(phi, y, sel, scale=None):
-    paths = y.shape[1]
-    width = min(256, paths)
-
-    def step(i, carry):
-        cut = pl.ds(pl.multiple_of(i * width, width), width)
-        rows = basis_chunk(y[:, cut], sel)
-        if scale is not None:
-            rows = rows * scale(cut)
-        phi[:, cut] = rows
-        return carry
-
-    lax.fori_loop(0, paths // width, step, 0)
-
-
-def pack(full):
-    rows = lax.broadcasted_iota(jnp.int32, (128, 128), 0)
-    lanes = lax.broadcasted_iota(jnp.int32, (128, 128), 1)
-    first = full[0:128, 0:128]
-    mixed = jnp.where(rows > lanes, first, full[128:256, 128:256])
-    diagonal = jnp.sum(jnp.where(rows == lanes, first, 0.0), axis=0, keepdims=True)
-    return full[0:128, 128:256], mixed, jnp.broadcast_to(diagonal, (8, 128))
-
-
-def unpack(cross, mixed, diagonal):
-    rows = lax.broadcasted_iota(jnp.int32, (128, 128), 0)
-    lanes = lax.broadcasted_iota(jnp.int32, (128, 128), 1)
-    turned = mixed.T
-    diagonal = jnp.broadcast_to(diagonal, (128, 128))
-    first = jnp.where(rows > lanes, mixed, jnp.where(rows < lanes, turned, diagonal))
-    last = jnp.where(rows <= lanes, mixed, turned)
-    return first, cross, cross.T, last
-
-
-def gram_kernel(states, flags, mean, inv, sel, out, y, phi):
-    d = pl.program_id(0)
-
-    @pl.when(d == 0)
-    def _():
-        fill_rest(y)
-
-    fill_factors(y, lambda cut: states[0, :, cut], mean[0], inv[0])
-    fill_basis(phi, y, sel, lambda cut: flags[pl.ds(d, 1), cut].astype(f32))
-    rows = phi[...]
-    full = lax.dot_general(
-        rows, rows, (((1,), (1,)), ((), ())), precision=HIGHEST, preferred_element_type=f32
-    )
-    cross, mixed, diagonal = pack(full)
-    out[0, 0:128, :] = cross
-    out[0, 128:256, :] = mixed
-    out[0, 256:264, :] = diagonal
-
-
-def gram_call(states, flags, mean, inv, sel):
-    paths = states.shape[2]
-    return pl.pallas_call(
-        gram_kernel,
-        name="gram",
-        grid=(DATES,),
-        out_shape=jax.ShapeDtypeStruct((DATES, PACKED, 128), f32),
-        in_specs=[
-            pl.BlockSpec((1, FACTORS, paths), lambda d: (d, 0, 0)),
-            pl.BlockSpec((DATES, paths), lambda d: (0, 0)),
-            pl.BlockSpec((1, 24, 128), lambda d: (d, 0, 0)),
-            pl.BlockSpec((1, 24, 128), lambda d: (d, 0, 0)),
-            pl.BlockSpec((2, 256, 96), lambda d: (0, 0, 0)),
-        ],
-        out_specs=pl.BlockSpec((1, PACKED, 128), lambda d: (d, 0, 0)),
-        scratch_shapes=[pltpu.VMEM((32, paths), f32), pltpu.VMEM((256, paths), f32)],
-    )(states, flags, mean, inv, sel)
-
-
-def collect_kernel(gram, out, slots, send_sem, recv_sem):
-    me = lax.axis_index("path")
-    barrier = greet(me)
-    pl.semaphore_wait(barrier, GROUP - 1)
-
-    def copy_of(d):
-        offset = lax.rem(me - OWNER[d] + GROUP, GROUP)
-        return pltpu.make_async_remote_copy(
-            src_ref=gram.at[d],
-            dst_ref=slots.at[offset],
-            send_sem=send_sem.at[d],
-            recv_sem=recv_sem.at[offset],
-            device_id={"path": OWNER[d]},
-            device_id_type=MESH_ID,
-        )
-
-    for d in range(DATES):
-
-        @pl.when(me != OWNER[d])
-        def _(d=d):
-            copy_of(d).start()
-
-    out[...] = jnp.zeros_like(out)
-    for d in range(DATES):
-
-        @pl.when(me == OWNER[d])
-        def _(d=d):
-            for k in range(1, GROUP):
-                pltpu.make_async_remote_copy(
-                    src_ref=gram.at[d],
-                    dst_ref=slots.at[k],
-                    send_sem=send_sem.at[d],
-                    recv_sem=recv_sem.at[k],
-                    device_id={"path": lax.rem(me + k, GROUP)},
-                    device_id_type=MESH_ID,
-                ).wait_recv()
-            total = gram[d]
-            for k in range(1, GROUP):
-                total = total + slots[k]
-            out[...] = total
-
-    for d in range(DATES):
-
-        @pl.when(me != OWNER[d])
-        def _(d=d):
-            copy_of(d).wait_send()
-
-
-def collect_call(gram):
-    return pl.pallas_call(
-        collect_kernel,
-        name="collect",
-        out_shape=jax.ShapeDtypeStruct((PACKED, 128), f32),
-        in_specs=[vmem()],
-        out_specs=vmem(),
-        scratch_shapes=[
-            pltpu.VMEM((GROUP, PACKED, 128), f32),
-            pltpu.SemaphoreType.DMA((DATES,)),
-            pltpu.SemaphoreType.DMA((GROUP,)),
-        ],
-        compiler_params=pltpu.CompilerParams(collective_id=1, has_side_effects=True),
-    )(gram)
+    )(states, flags, sel)
 
 
 def sweep_block(panel, b, start):
@@ -329,14 +429,10 @@
     return jnp.concatenate(pieces, axis=0)
 
 
-def inverse_kernel(gram, count, out, work):
-    scale = 1.0 / count[0:1, :]
-    rows = lax.broadcasted_iota(jnp.int32, (128, 128), 0)
-    lanes = lax.broadcasted_iota(jnp.int32, (128, 128), 1)
+def inverse_kernel(gram, out, work):
+    rows, lanes = triangle()
     ridge = jnp.where(rows == lanes, RIDGE, 0.0).astype(f32)
-    first, cross, turned, last = unpack(
-        gram[0:128, :] * scale, gram[128:256, :] * scale, gram[256:257, :] * scale
-    )
+    first, cross, turned, last = unpack(gram[0:128, :], gram[128:256, :], gram[256:257, :])
     work[0:128, 0:128] = first + ridge
     work[0:128, 128:256] = cross
     work[128:256, 0:128] = turned
@@ -358,28 +454,28 @@
         )
         work[...] = jnp.where((lane >= top) & (lane < top + deep), 0.0, work[...]) - change
         work[top : top + deep, :] = panel
-    cross, mixed, diagonal = pack(-work[...])
-    out[0:128, :] = cross
+    mixed, diagonal = pack(-work[0:128, 0:128], -work[128:256, 128:256])
+    out[0:128, :] = -work[0:128, 128:256]
     out[128:256, :] = mixed
     out[256:264, :] = diagonal
 
 
-def inverse_call(gram, count):
+def inverse_call(gram):
     return pl.pallas_call(
         inverse_kernel,
         name="inverse",
         out_shape=jax.ShapeDtypeStruct((PACKED, 128), f32),
-        in_specs=[vmem()] * 2,
+        in_specs=[vmem()],
         out_specs=vmem(),
         scratch_shapes=[pltpu.VMEM((256, 256), f32)],
-    )(gram, count)
+    )(gram)
 
 
 def chain_kernel(
     states, flags, terminal, strike, date_index, mean, inv, count, sel, mine,
     cash_out, price_out, coef_out,
     y, phi, exercise, discount, value, packed, solve, slots, slots_price, coefs,
-    bulk_send, bulk_recv, send_sem, recv_sem, price_send, price_recv,
+    spread_send, spread_recv, send_sem, recv_sem, price_send, price_recv,
 ):
     me = lax.axis_index("path")
     barrier = greet(me)
@@ -405,15 +501,30 @@
             exercise[par, :, cut] = 100.0 * annuity * (rate - strike[0])
         fill_basis(phi.at[par], y, sel)
 
-    def bulk(d, k):
+    my_z, my_x = me // SIDE, lax.rem(me, SIDE)
+    spans = (slice(0, HALF), slice(HALF, PACKED))
+
+    def along(axis, k):
+        if axis == 0:
+            return {"path": my_z * SIDE + lax.rem(my_x + k, SIDE)}
+        return {"path": lax.rem(my_z + k, SIDE) * SIDE + my_x}
+
+    def spread(source, d, half, axis, k, stage):
         return pltpu.make_async_remote_copy(
-            src_ref=mine,
-            dst_ref=packed.at[d],
-            send_sem=bulk_send.at[k],
-            recv_sem=bulk_recv.at[d],
-            device_id={"path": lax.rem(me + k, GROUP)},
+            src_ref=source,
+            dst_ref=packed.at[d, spans[half]],
+            send_sem=spread_send.at[stage, half, d // SIDE, k],
+            recv_sem=spread_recv.at[half, d],
+            device_id=along(axis, k),
             device_id_type=MESH_ID,
         )
+
+    def relay(d, half):
+        apart = my_z != owner_z(d) if half == 0 else my_x != owner_x(d)
+        return jnp.logical_not(apart)
+
+    def is_owner(d):
+        return (my_x == owner_x(d)) & (my_z == owner_z(d))
 
     def rhs_copy(par, k):
         return pltpu.make_async_remote_copy(
@@ -437,29 +548,36 @@
 
     fill_rest(y)
     pl.semaphore_wait(barrier, GROUP - 1)
-    for d in range(DATES):
-
-        @pl.when(me == OWNER[d])
-        def _(d=d):
-            for k in range(1, GROUP):
-                bulk(d, k).start()
-            packed[d] = mine[...]
+    own_q = lax.rem(my_z - my_x + SIDE, SIDE)
+    own = own_q * SIDE + my_x
+
+    @pl.when(own < DATES)
+    def _():
+        for k in range(1, SIDE):
+            for half in range(2):
+                spread(mine.at[spans[half]], own, half, half, k, 0).start()
+        for k in range(1, SIDE):
+            for half in range(2):
+                spread(mine.at[spans[half]], own, half, 1 - half, k, 1).start()
+        packed[own] = mine[...]
 
     prepare(DATES - 1, 0)
     value[...] = terminal[...]
     coefs[...] = jnp.zeros_like(coefs)
-    for d in range(DATES):
-
-        @pl.when(me != OWNER[d])
-        def _(d=d):
-            bulk(d, 1).wait_recv()
-
-    for d in range(DATES):
-
-        @pl.when(me == OWNER[d])
-        def _(d=d):
-            for k in range(1, GROUP):
-                bulk(d, k).wait_send()
+    def relay_step(t, carry):
+        d = DATES - 1 - t
+        for half in range(2):
+
+            @pl.when(relay(d, half) & jnp.logical_not(is_owner(d)))
+            def _(half=half):
+                source = packed.at[d, spans[half]]
+                spread(source, d, half, half, 1, 0).wait_recv()
+                for k in range(1, SIDE):
+                    spread(source, d, half, 1 - half, k, 1).start()
+
+        return carry
+
+    lax.fori_loop(0, DATES, relay_step, 0)
 
     def date_step(t, carry):
         d = DATES - 1 - t
@@ -478,6 +596,12 @@
         slots[par, me] = jnp.concatenate([low, high], axis=0)
         for k in range(1, GROUP):
             rhs_copy(par, k).start()
+
+        for half in range(2):
+
+            @pl.when(jnp.logical_not(relay(d, half)))
+            def _(half=half):
+                spread(packed.at[d, spans[half]], d, half, half, 1, 0).wait_recv()
 
         first, cross, turned, last = unpack(
             packed[d, 0:128, :], packed[d, 128:256, :], packed[d, 256:257, :]
@@ -531,6 +655,25 @@
     price_out[...] = jnp.broadcast_to(price, (1, 128))
     for k in range(1, GROUP):
         price_copy(k).wait_send()
+
+    @pl.when(own < DATES)
+    def _():
+        for k in range(1, SIDE):
+            for half in range(2):
+                spread(mine.at[spans[half]], own, half, half, k, 0).wait_send()
+                spread(mine.at[spans[half]], own, half, 1 - half, k, 1).wait_send()
+
+    def relay_done(d, carry):
+        for half in range(2):
+
+            @pl.when(relay(d, half) & jnp.logical_not(is_owner(d)))
+            def _(half=half):
+                for k in range(1, SIDE):
+                    spread(packed.at[d, spans[half]], d, half, 1 - half, k, 1).wait_send()
+
+        return carry
+
+    lax.fori_loop(0, DATES, relay_done, 0)
 
 
 def chain_call(states, flags, terminal, strike, date_index, mean, inv, count, sel, mine):
@@ -556,8 +699,8 @@
             pltpu.VMEM((2, GROUP, 2, 128), f32),
             pltpu.VMEM((GROUP, 1, 128), f32),
             pltpu.VMEM((256, 128), f32),
-            pltpu.SemaphoreType.DMA((GROUP,)),
-            pltpu.SemaphoreType.DMA((DATES,)),
+            pltpu.SemaphoreType.DMA((2, 2, DATES // SIDE + 1, SIDE)),
+            pltpu.SemaphoreType.DMA((2, DATES)),
             pltpu.SemaphoreType.DMA((2, GROUP)),
             pltpu.SemaphoreType.DMA((2, GROUP)),
             pltpu.SemaphoreType.DMA((GROUP,)),
@@ -570,14 +713,8 @@
 def shards(states, flags, terminal, strike, date_index):
     paths = states.shape[2]
     sel = selectors()
-    mean, inv, count = stats_call(states, flags)
-    gram = gram_call(states, flags, mean, inv, sel)
-    mine = collect_call(gram)
-    me = lax.axis_index("path")
-    own_count = count[0]
-    for d in range(1, DATES):
-        own_count = jnp.where(me == OWNER[d], count[d], own_count)
-    packed = inverse_call(mine, own_count)
+    mean, inv, count, system = front_call(states, flags, sel)
+    packed = inverse_call(system)
     cash, price, coefs = chain_call(
         states, flags, terminal.reshape(1, paths), strike, date_index.reshape(1, paths),
         mean, inv, count, sel, packed,

time: 200 us -> 145 us (0.72)
  Pallas kernels: 194 us -> 139 us
    pallas_call x3 -> x1, Pallas kernels: 80.5 us -> 50.1 us  [front_call(): pl.pallas_call(front_kernel, name='front', out_shape=(jax.ShapeDtypeStruc...]
    pallas_call x1, Pallas kernels: 100 us -> 75.8 us  [chain_call(): pl.pallas_call(chain_kernel, name='chain', out_shape=(jax.ShapeDtypeStruc...]
where the time goes in v2:
time: 145 us; the launch traced here: 144 us
  Pallas kernels  139 us (96%)
  between operations  3.12 us (2%)
  local copies, waits for them, and re-layouts  2.62 us (2%)
    pallas_call x1, Pallas kernels, chain_call(): pl.pallas_call(chain_kernel, name='chain', out_shape=(jax.ShapeDtypeStruc...  75.8 us
    pallas_call x1, Pallas kernels, front_call(): pl.pallas_call(front_kernel, name='front', out_shape=(jax.ShapeDtypeStruc...  50.1 us
    pallas_call x1, Pallas kernels, inverse_call(): pl.pallas_call(inverse_kernel, name='inverse', out_shape=jax.ShapeDtypeSt...  12.8 us

profile of v2, /device:TPU:0, one launch (start us, length us, event | category | flops | bytes accessed | tf_op | source)
XLA Modules:
  0.0 144.4 jit_solution(3535786500374670762)
XLA Ops:
  0.6 50.1 %front.1 = (f32[10,24,128]{2,1,0:T(8,128)}, f32[10,24,128]{2,1,0:T(8,128)}, f32[10,8,128]{2,1,0:T(8,128)}, f32[264,128]{1,0:T(8,128)}) custom-call(f32[10,20,2048]{2,1,0:T(8,128)} %states.3, s32[10,2048]{1,0:T(8,128)} %flags.3, bf16[2,256,96]{2,1,0:T(8,128)(2,1)} %constant.2.clone.sel), custom_call_target="tpu_custom_call" | custom-call | tf_op jit(solution)/shard_map/front/pallas_call | solution.py:358
  50.7 12.8 %inverse.1.mine = f32[264,128]{1,0:T(8,128)} custom-call(f32[264,128]{1,0:T(8,128)} %get-tuple-element.13.gram), custom_call_target="tpu_custom_call" | custom-call | tf_op jit(solution)/shard_map/inverse/pallas_call | solution.py:464
  64.2 75.8 %chain.1 = (f32[1,2048]{1,0:T(1,128)}, f32[1,128]{1,0:T(1,128)}, f32[10,231]{1,0:T(8,128)}) custom-call(f32[10,20,2048]{2,1,0:T(8,128)} %states.3, s32[10,2048]{1,0:T(8,128)} %flags.3, f32[1,2048]{1,0:T(1,128)} %bitcast.5, f32[1]{0:T(128)S(6)} %copy.12.strike, s32[1,2048]{1,0:T(1,128)} %bitcast.6, f32[10,24,128]{2,1,0:T(8,128)} %get-tuple-element.10.mean, ...), custom_call_target="tpu_custom_call" | custom-call | tf_op jit(solution)/shard_map/chain/pallas_call | solution.py:681
  140.0 1.3 copy.13
  142.0 1.3 copy.15

commit v3 on v2

--- a/solution.py
+++ b/solution.py
@@ -25,16 +25,31 @@
 MESH_ID = pl.DeviceIdType.MESH
 
 
-def selectors():
+def basis_pairs():
+    pairs = []
+    for base in (0, 8):
+        for s in range(4):
+            pairs += [(base + i, base + (i + s) % 8) for i in range(8)]
+    pairs += [(i, i + 4) for i in range(4)] + [(8 + i, 8 + (i + 4) % 8) for i in range(4, 8)]
+    for s in range(8):
+        pairs += [(i, 8 + (i + s) % 8) for i in range(8)]
+    for base in (0, 8):
+        for k in range(5):
+            pairs += [(base + i, 16 + k) for i in range(8)]
+    pairs += [(16 + i, 16 + i) for i in range(5)] + [(16 + i, 18 + i) for i in range(3)]
+    pairs += [(16 + i, 17 + i) for i in range(4)] + [(16, 19), (17, 20), (16, 20)]
+    return [tuple(sorted(pair)) for pair in pairs]
+
+
+def reference_order():
     left, right = np.triu_indices(FACTORS)
-    pairs = [(FACTORS, FACTORS)] + [(j, FACTORS) for j in range(FACTORS)]
-    pairs += list(zip(left.tolist(), right.tolist()))
-    sel = np.zeros((2, 256, 96), np.float32)
-    for row, (a, b) in enumerate(pairs):
-        for part in range(3):
-            sel[0, row, 32 * part + a] = 1.0
-            sel[1, row, 32 * part + b] = 1.0
-    return jnp.asarray(sel, bf16)
+    wanted = [(FACTORS, FACTORS)] + [(j, FACTORS) for j in range(FACTORS)]
+    wanted += list(zip(left.tolist(), right.tolist()))
+    held = basis_pairs()
+    move = np.zeros((256, 256), np.float32)
+    for column, pair in enumerate(wanted):
+        move[held.index(pair), column] = 1.0
+    return jnp.asarray(move, bf16)
 
 
 def owner_x(d):
@@ -76,31 +91,43 @@
 def fill_rest(y):
     paths = y.shape[1]
     y[FACTORS : FACTORS + 1, :] = jnp.ones((1, paths), f32)
-    y[FACTORS + 1 : 32, :] = jnp.zeros((31 - FACTORS, paths), f32)
-
-
-def basis_chunk(y_chunk, sel):
-    stacked = jnp.concatenate(three_parts(y_chunk), axis=0)
-    left = jnp.dot(sel[0], stacked, preferred_element_type=f32)
-    right = jnp.dot(sel[1], stacked, preferred_element_type=f32)
-    return left * right
-
-
-def over_chunks(paths, body):
-    width = min(256, paths)
+    y[FACTORS + 1 : 24, :] = jnp.zeros((23 - FACTORS, paths), f32)
+
+
+def turn(rows, s):
+    return rows if s == 0 else pltpu.roll(rows, 8 - s, 0)
+
+
+def products(y_chunk, money=None):
+    groups = [y_chunk[8 * g : 8 * g + 8, :] for g in range(3)]
+    scaled = groups if money is None else [group * money for group in groups]
+    turned = [turn(groups[1], s) for s in range(8)]
+    pieces = [scaled[0] * turn(groups[0], s) for s in range(4)]
+    pieces += [scaled[1] * turned[s] for s in range(4)]
+    row = lax.broadcasted_iota(jnp.int32, groups[0].shape, 0)
+    left = jnp.where(row < 4, scaled[0], scaled[1])
+    pieces.append(left * jnp.where(row < 4, turn(groups[0], 4), turned[4]))
+    pieces += [scaled[0] * turned[s] for s in range(8)]
+    single = [jnp.broadcast_to(groups[2][k : k + 1, :], groups[0].shape) for k in range(5)]
+    for g in range(2):
+        pieces += [scaled[g] * single[k] for k in range(5)]
+    apart = [scaled[2] * turn(groups[2], s) for s in range(5)]
+    pieces.append(apart[0] + pltpu.roll(apart[2], 5, 0))
+    ends = jnp.where(row < 4, apart[4], 0.0)
+    pieces.append(apart[1] + pltpu.roll(apart[3], 4, 0) + pltpu.roll(ends, 6, 0))
+    return pieces
+
+
+def fill_basis(phi, y):
+    paths = y.shape[1]
 
     def step(i, carry):
-        body(pl.ds(pl.multiple_of(i * width, width), width))
+        cut = pl.ds(pl.multiple_of(i * 128, 128), 128)
+        for q, piece in enumerate(products(y[:, cut])):
+            phi[8 * q : 8 * q + 8, cut] = piece
         return carry
 
-    lax.fori_loop(0, paths // width, step, 0)
-
-
-def fill_basis(phi, y, sel):
-    def body(cut):
-        phi[:, cut] = basis_chunk(y[:, cut], sel)
-
-    over_chunks(y.shape[1], body)
+    lax.fori_loop(0, paths // 128, step, 0)
 
 
 def triangle():
@@ -131,8 +158,8 @@
 
 
 def front_kernel(
-    states, flags, sel, mean_out, inv_out, count_out, system_out,
-    part, slots, y, parts, gram, slot_a, slot_b, sum_a, sum_b, last_a, last_b,
+    states, flags, mean_out, inv_out, count_out, system_out,
+    part, slots, money_of, y, parts_0, parts_1, gram, slot_a, slot_b, sum_a, sum_b, last_a, last_b,
     send_sem, recv_sem, send_a, send_b, recv_a, recv_b,
     send_last_a, send_last_b, recv_last_a, recv_last_b,
 ):
@@ -147,6 +174,7 @@
         for c in range(paths // 128):
             z = states[d, :, 128 * c : 128 * c + 128]
             m = flags[d : d + 1, 128 * c : 128 * c + 128].astype(f32)
+            money_of[d, :, 128 * c : 128 * c + 128] = m
             mz = m * z
             first = first + mz
             second = second + mz * z
@@ -234,24 +262,31 @@
             device_id_type=MESH_ID,
         )
 
-    def compute(d):
+    def split(d, parts):
         fill_factors(y, lambda cut: states[d, :, cut], mean_out[d], inv_out[d])
-
-        def body(cut):
-            rows = basis_chunk(y[:, cut], sel) * flags[pl.ds(d, 1), cut].astype(f32)
-            one, two, three = three_parts(rows)
-            parts[0:256, cut] = one
-            parts[256:512, cut] = two
-            parts[512:768, cut] = three
-
-        over_chunks(paths, body)
+        for c in range(paths // 128):
+            cut = slice(128 * c, 128 * c + 128)
+            money = money_of[d, :, cut]
+            pieces = products(y[:, cut], money)
+            pieces.append(jnp.zeros((8, 128), f32))
+            for q in range(0, 30, 2):
+                rows = jnp.concatenate(pieces[q : q + 2], axis=0)
+                for i, piece in enumerate(three_parts(rows)):
+                    parts[c, 256 * i + 8 * q : 256 * i + 8 * q + 16, :] = piece
+
+    def compute(d, parts, other):
         lanes = (((1,), (1,)), ((), ()))
-        wide = lax.dot_general(parts[0:256, :], parts[...], lanes, preferred_element_type=f32)
-        small = lax.dot_general(
-            parts[256:512, :], parts[256:512, :], lanes, preferred_element_type=f32
-        )
-        main = wide[:, 0:256] + small
-        side = wide[:, 256:512] + wide[:, 512:768]
+        whole = [
+            jnp.concatenate(
+                [parts[c, 256 * i : 256 * i + 256, :] for c in range(paths // 128)], axis=1
+            )
+            for i in range(3)
+        ]
+        main = lax.dot_general(whole[0], whole[0], lanes, preferred_element_type=f32)
+        main = main + lax.dot_general(whole[1], whole[1], lanes, preferred_element_type=f32)
+        side = lax.dot_general(whole[0], whole[1], lanes, preferred_element_type=f32)
+        side = side + lax.dot_general(whole[0], whole[2], lanes, preferred_element_type=f32)
+        split(jnp.minimum(d + 1, DATES - 1), other)
         low, high = slice(0, 128), slice(128, 256)
         gram[d, 0:128, :] = main[low, high] + (side[low, high] + side[high, low].T)
         mixed, diagonal = pack(
@@ -298,17 +333,23 @@
             def _():
                 last_copy_b(d, k_x).start()
 
-    def date_step(d, carry):
-        compute(d)
-        send(d)
-
-        @pl.when(d >= LAG)
-        def _():
-            collect(d - LAG)
+    def two_dates(i, carry):
+        for half, parts, other in ((0, parts_0, parts_1), (1, parts_1, parts_0)):
+            d = 2 * i + half
+            compute(d, parts, other)
+            send(d)
+
+            @pl.when(d >= LAG)
+            def _(d=d):
+                collect(d - LAG)
 
         return carry
 
-    lax.fori_loop(0, DATES, date_step, 0)
+    for parts in (parts_0, parts_1):
+        for i in range(3):
+            parts[:, 256 * i + 240 : 256 * i + 256, :] = jnp.zeros((paths // 128, 16, 128), bf16)
+    split(0, parts_0)
+    lax.fori_loop(0, DATES // 2, two_dates, 0)
     lax.fori_loop(DATES - LAG, DATES, lambda d, carry: (collect(d), carry)[1], 0)
 
     own_q = lax.rem(my_z - my_x + SIDE, SIDE)
@@ -351,7 +392,7 @@
         copy.wait_send()
 
 
-def front_call(states, flags, sel):
+def front_call(states, flags):
     paths = states.shape[2]
     columns = DATES // SIDE + 1
     dma = pltpu.SemaphoreType.DMA
@@ -364,13 +405,15 @@
             jax.ShapeDtypeStruct((DATES, 8, 128), f32),
             jax.ShapeDtypeStruct((PACKED, 128), f32),
         ),
-        in_specs=[vmem()] * 3,
+        in_specs=[vmem()] * 2,
         out_specs=(vmem(),) * 4,
         scratch_shapes=[
             pltpu.VMEM((640, 128), f32),
             pltpu.VMEM((GROUP, 8, 128), f32),
-            pltpu.VMEM((32, paths), f32),
-            pltpu.VMEM((768, paths), bf16),
+            pltpu.VMEM((DATES, 1, paths), f32),
+            pltpu.VMEM((24, paths), f32),
+            pltpu.VMEM((paths // 128, 768, 128), bf16),
+            pltpu.VMEM((paths // 128, 768, 128), bf16),
             pltpu.VMEM((DATES, PACKED, 128), f32),
             pltpu.VMEM((columns, SIDE, HALF, 128), f32),
             pltpu.VMEM((columns, SIDE, PACKED - HALF, 128), f32),
@@ -390,7 +433,7 @@
             dma((SIDE,)),
         ],
         compiler_params=pltpu.CompilerParams(collective_id=0, has_side_effects=True),
-    )(states, flags, sel)
+    )(states, flags)
 
 
 def sweep_block(panel, b, start):
@@ -472,7 +515,7 @@
 
 
 def chain_kernel(
-    states, flags, terminal, strike, date_index, mean, inv, count, sel, mine,
+    states, flags, terminal, strike, date_index, mean, inv, count, mine, move,
     cash_out, price_out, coef_out,
     y, phi, exercise, discount, value, packed, solve, slots, slots_price, coefs,
     spread_send, spread_recv, send_sem, recv_sem, price_send, price_recv,
@@ -499,7 +542,7 @@
             annuity = 0.25 * total
             rate = (1.0 - running) / annuity
             exercise[par, :, cut] = 100.0 * annuity * (rate - strike[0])
-        fill_basis(phi.at[par], y, sel)
+        fill_basis(phi.at[par], y)
 
     my_z, my_x = me // SIDE, lax.rem(me, SIDE)
     spans = (slice(0, HALF), slice(HALF, PACKED))
@@ -645,7 +688,10 @@
         price_copy(k).start()
     cash_out[...] = value[...]
     turned = jnp.concatenate([coefs[0:128, :].T[0:16, :], coefs[128:256, :].T[0:16, :]], axis=1)
-    coef_out[...] = turned[0:DATES, 0:BASIS]
+    ordered = jnp.zeros((16, 256), f32)
+    for piece in three_parts(turned)[::-1]:
+        ordered = ordered + jnp.dot(piece, move[...], preferred_element_type=f32)
+    coef_out[...] = ordered[0:DATES, 0:BASIS]
     for k in range(1, GROUP):
         price_copy(k).wait_recv()
     total = slots_price[0]
@@ -676,7 +722,7 @@
     lax.fori_loop(0, DATES, relay_done, 0)
 
 
-def chain_call(states, flags, terminal, strike, date_index, mean, inv, count, sel, mine):
+def chain_call(states, flags, terminal, strike, date_index, mean, inv, count, mine, move):
     paths = states.shape[2]
     return pl.pallas_call(
         chain_kernel,
@@ -689,8 +735,8 @@
         in_specs=[vmem()] * 3 + [pl.BlockSpec(memory_space=pltpu.SMEM)] + [vmem()] * 6,
         out_specs=(vmem(),) * 3,
         scratch_shapes=[
-            pltpu.VMEM((32, paths), f32),
-            pltpu.VMEM((2, 256, paths), f32),
+            pltpu.VMEM((24, paths), f32),
+            pltpu.VMEM((2, ROWS, paths), f32),
             pltpu.VMEM((2, 1, paths), f32),
             pltpu.VMEM((2, 1, paths), f32),
             pltpu.VMEM((1, paths), f32),
@@ -707,17 +753,16 @@
             pltpu.SemaphoreType.DMA((GROUP,)),
         ],
         compiler_params=pltpu.CompilerParams(collective_id=2, has_side_effects=True),
-    )(states, flags, terminal, strike, date_index, mean, inv, count, sel, mine)
+    )(states, flags, terminal, strike, date_index, mean, inv, count, mine, move)
 
 
 def shards(states, flags, terminal, strike, date_index):
     paths = states.shape[2]
-    sel = selectors()
-    mean, inv, count, system = front_call(states, flags, sel)
+    mean, inv, count, system = front_call(states, flags)
     packed = inverse_call(system)
     cash, price, coefs = chain_call(
         states, flags, terminal.reshape(1, paths), strike, date_index.reshape(1, paths),
-        mean, inv, count, sel, packed,
+        mean, inv, count, packed, reference_order(),
     )
     return cash.reshape(paths), price[0, 0:1], coefs
 

time: 145 us -> 134 us (0.924)
  Pallas kernels: 139 us -> 128 us
    pallas_call x1, Pallas kernels: 50.1 us -> 39.5 us  [front_call(): pl.pallas_call(front_kernel, name='front', out_shape=(jax.ShapeDtypeStruc...]
where the time goes in v3:
time: 134 us
  Pallas kernels  128 us (96%)
  between operations  3.12 us (2%)
  local copies, waits for them, and re-layouts  2.62 us (2%)
    pallas_call x1, Pallas kernels, chain_call(): pl.pallas_call(chain_kernel, name='chain', out_shape=(jax.ShapeDtypeStruc...  75.6 us
    pallas_call x1, Pallas kernels, front_call(): pl.pallas_call(front_kernel, name='front', out_shape=(jax.ShapeDtypeStruc...  39.5 us
    pallas_call x1, Pallas kernels, inverse_call(): pl.pallas_call(inverse_kernel, name='inverse', out_shape=jax.ShapeDtypeSt...  12.8 us

profile of v3, /device:TPU:0, one launch (start us, length us, event | category | flops | bytes accessed | tf_op | source)
XLA Modules:
  0.0 133.6 jit_solution(2658860659430777684)
XLA Ops:
  0.6 39.5 %front.1 = (f32[10,24,128]{2,1,0:T(8,128)}, f32[10,24,128]{2,1,0:T(8,128)}, f32[10,8,128]{2,1,0:T(8,128)}, f32[264,128]{1,0:T(8,128)}) custom-call(f32[10,20,2048]{2,1,0:T(8,128)} %states.3, s32[10,2048]{1,0:T(8,128)} %flags.3), custom_call_target="tpu_custom_call" | custom-call | tf_op jit(solution)/shard_map/front/pallas_call | solution.py:399
  40.1 12.8 %inverse.1.mine = f32[264,128]{1,0:T(8,128)} custom-call(f32[264,128]{1,0:T(8,128)} %get-tuple-element.13.gram), custom_call_target="tpu_custom_call" | custom-call | tf_op jit(solution)/shard_map/inverse/pallas_call | solution.py:507
  53.6 75.6 %chain.1 = (f32[1,2048]{1,0:T(1,128)}, f32[1,128]{1,0:T(1,128)}, f32[10,231]{1,0:T(8,128)}) custom-call(f32[10,20,2048]{2,1,0:T(8,128)} %states.3, s32[10,2048]{1,0:T(8,128)} %flags.3, f32[1,2048]{1,0:T(1,128)} %bitcast.5, f32[1]{0:T(128)S(6)} %copy.12.strike, s32[1,2048]{1,0:T(1,128)} %bitcast.6, f32[10,24,128]{2,1,0:T(8,128)} %get-tuple-element.10.mean, ...), custom_call_target="tpu_custom_call" | custom-call | tf_op jit(solution)/shard_map/chain/pallas_call | solution.py:727
  129.2 1.3 copy.13
  131.2 1.3 copy.15

commit v4 on v3

--- a/solution.py
+++ b/solution.py
@@ -22,6 +22,7 @@
 HALF = 136
 SIDE = 4
 LAG = 2
+CHUNKS = 8
 MESH_ID = pl.DeviceIdType.MESH
 
 
@@ -159,7 +160,7 @@
 
 def front_kernel(
     states, flags, mean_out, inv_out, count_out, system_out,
-    part, slots, money_of, y, parts_0, parts_1, gram, slot_a, slot_b, sum_a, sum_b, last_a, last_b,
+    part, slots, money_of, y, parts, gram, slot_a, slot_b, sum_a, sum_b, last_a, last_b,
     send_sem, recv_sem, send_a, send_b, recv_a, recv_b,
     send_last_a, send_last_b, recv_last_a, recv_last_b,
 ):
@@ -262,10 +263,10 @@
             device_id_type=MESH_ID,
         )
 
-    def split(d, parts):
-        fill_factors(y, lambda cut: states[d, :, cut], mean_out[d], inv_out[d])
-        for c in range(paths // 128):
+    def split(d, parts, slabs):
+        for c in slabs:
             cut = slice(128 * c, 128 * c + 128)
+            y[0:FACTORS, cut] = (states[d, :, cut] - mean_out[d, 0:FACTORS]) * inv_out[d, 0:FACTORS]
             money = money_of[d, :, cut]
             pieces = products(y[:, cut], money)
             pieces.append(jnp.zeros((8, 128), f32))
@@ -274,19 +275,29 @@
                 for i, piece in enumerate(three_parts(rows)):
                     parts[c, 256 * i + 8 * q : 256 * i + 8 * q + 16, :] = piece
 
-    def compute(d, parts, other):
+    def compute(d, parts):
         lanes = (((1,), (1,)), ((), ()))
-        whole = [
-            jnp.concatenate(
-                [parts[c, 256 * i : 256 * i + 256, :] for c in range(paths // 128)], axis=1
-            )
-            for i in range(3)
-        ]
-        main = lax.dot_general(whole[0], whole[0], lanes, preferred_element_type=f32)
-        main = main + lax.dot_general(whole[1], whole[1], lanes, preferred_element_type=f32)
-        side = lax.dot_general(whole[0], whole[1], lanes, preferred_element_type=f32)
-        side = side + lax.dot_general(whole[0], whole[2], lanes, preferred_element_type=f32)
-        split(jnp.minimum(d + 1, DATES - 1), other)
+        total = paths // 128
+        step = max(total // CHUNKS, 1)
+        main = jnp.zeros((256, 256), f32)
+        side = jnp.zeros((256, 256), f32)
+        for start in range(0, total, step):
+            slabs = range(start, start + step)
+            split(d, parts, slabs)
+            whole = [
+                jnp.concatenate(
+                    [parts[c, 256 * i : 256 * i + 256, :] for c in slabs], axis=1
+                )
+                for i in range(3)
+            ]
+            for i, k in ((0, 0), (1, 1)):
+                main = main + lax.dot_general(
+                    whole[i], whole[k], lanes, preferred_element_type=f32
+                )
+            for i, k in ((0, 1), (0, 2)):
+                side = side + lax.dot_general(
+                    whole[i], whole[k], lanes, preferred_element_type=f32
+                )
         low, high = slice(0, 128), slice(128, 256)
         gram[d, 0:128, :] = main[low, high] + (side[low, high] + side[high, low].T)
         mixed, diagonal = pack(
@@ -333,23 +344,19 @@
             def _():
                 last_copy_b(d, k_x).start()
 
-    def two_dates(i, carry):
-        for half, parts, other in ((0, parts_0, parts_1), (1, parts_1, parts_0)):
-            d = 2 * i + half
-            compute(d, parts, other)
-            send(d)
-
-            @pl.when(d >= LAG)
-            def _(d=d):
-                collect(d - LAG)
+    def date_step(d, carry):
+        compute(d, parts)
+        send(d)
+
+        @pl.when(d >= LAG)
+        def _():
+            collect(d - LAG)
 
         return carry
 
-    for parts in (parts_0, parts_1):
-        for i in range(3):
-            parts[:, 256 * i + 240 : 256 * i + 256, :] = jnp.zeros((paths // 128, 16, 128), bf16)
-    split(0, parts_0)
-    lax.fori_loop(0, DATES // 2, two_dates, 0)
+    for i in range(3):
+        parts[:, 256 * i + 240 : 256 * i + 256, :] = jnp.zeros((paths // 128, 16, 128), bf16)
+    lax.fori_loop(0, DATES, date_step, 0)
     lax.fori_loop(DATES - LAG, DATES, lambda d, carry: (collect(d), carry)[1], 0)
 
     own_q = lax.rem(my_z - my_x + SIDE, SIDE)
@@ -412,7 +419,6 @@
             pltpu.VMEM((GROUP, 8, 128), f32),
             pltpu.VMEM((DATES, 1, paths), f32),
             pltpu.VMEM((24, paths), f32),
-            pltpu.VMEM((paths // 128, 768, 128), bf16),
             pltpu.VMEM((paths // 128, 768, 128), bf16),
             pltpu.VMEM((DATES, PACKED, 128), f32),
             pltpu.VMEM((columns, SIDE, HALF, 128), f32),
@@ -472,6 +478,20 @@
     return jnp.concatenate(pieces, axis=0)
 
 
+def stacked(before, panel):
+    one, two, three = three_parts(before)
+    uno, due, tre = three_parts(panel)
+    left = jnp.concatenate([three, two, one, two, one, one], axis=0)
+    right = jnp.concatenate([uno, due, tre, uno, due, uno], axis=0)
+    return left, right
+
+
+def transposed_product(left, right):
+    return lax.dot_general(
+        left, right, (((0,), (0,)), ((), ())), preferred_element_type=f32
+    )
+
+
 def inverse_kernel(gram, out, work):
     rows, lanes = triangle()
     ridge = jnp.where(rows == lanes, RIDGE, 0.0).astype(f32)
@@ -480,23 +500,26 @@
     work[0:128, 128:256] = cross
     work[128:256, 0:128] = turned
     work[128:256, 128:256] = last + ridge
+    lane = lax.broadcasted_iota(jnp.int32, (256, 256), 1)
+    current = work[0:32, :]
     for top in range(0, ROWS, 32):
-        before = work[top : top + 32, :]
+        before = current
         panel = before
         for b in range(4):
             if top + 8 * b < ROWS:
                 panel = sweep_block(panel, b, top + 8 * b)
-        if top + 32 > ROWS:
-            keep = ROWS - top
-            before = before[0:keep, :]
-            panel = panel[0:keep, :]
-        deep = before.shape[0]
-        lane = lax.broadcasted_iota(jnp.int32, (256, 256), 1)
-        change = lax.dot_general(
-            before, panel, (((0,), (0,)), ((), ())), precision=HIGHEST, preferred_element_type=f32
-        )
-        work[...] = jnp.where((lane >= top) & (lane < top + deep), 0.0, work[...]) - change
-        work[top : top + deep, :] = panel
+        deep = min(32, ROWS - top)
+        if deep < 32:
+            row = lax.broadcasted_iota(jnp.int32, (32, 256), 0)
+            before = jnp.where(row < deep, before, 0.0)
+        kept = (lane < top) | (lane >= top + deep)
+        after = top + 32
+        left, right = stacked(before, panel)
+        if after < ROWS:
+            change = transposed_product(left[:, after : after + 32], right)
+            current = jnp.where(kept[0:32, :], work[after : after + 32, :], 0.0) - change
+        work[...] = jnp.where(kept, work[...], 0.0) - transposed_product(left, right)
+        work[top : top + deep, :] = panel[0:deep, :]
     mixed, diagonal = pack(-work[0:128, 0:128], -work[128:256, 128:256])
     out[0:128, :] = -work[0:128, 128:256]
     out[128:256, :] = mixed

time: 134 us -> 128 us (0.955)
  Pallas kernels: 128 us -> 122 us
    pallas_call x1, Pallas kernels: 12.8 us -> 10 us  [inverse_call(): pl.pallas_call(inverse_kernel, name='inverse', out_shape=jax.ShapeDtypeSt...]
    pallas_call x1, Pallas kernels: 39.5 us -> 36.9 us  [front_call(): pl.pallas_call(front_kernel, name='front', out_shape=(jax.ShapeDtypeStruc...]
where the time goes in v4:
time: 128 us; the launch traced here: 127 us
  Pallas kernels  122 us (95%)
  between operations  3.12 us (2%)
  local copies, waits for them, and re-layouts  2.62 us (2%)
    pallas_call x1, Pallas kernels, chain_call(): pl.pallas_call(chain_kernel, name='chain', out_shape=(jax.ShapeDtypeStruc...  74.9 us
    pallas_call x1, Pallas kernels, front_call(): pl.pallas_call(front_kernel, name='front', out_shape=(jax.ShapeDtypeStruc...  36.9 us
    pallas_call x1, Pallas kernels, inverse_call(): pl.pallas_call(inverse_kernel, name='inverse', out_shape=jax.ShapeDtypeSt...  10 us
    unnamed x2, local copies, waits for them, and re-layouts  2.62 us

profile of v4, /device:TPU:0, one launch (start us, length us, event | category | flops | bytes accessed | tf_op | source)
XLA Modules:
  0.0 127.5 jit_solution(12966356686174444394)
XLA Ops:
  0.6 36.9 %front.1 = (f32[10,24,128]{2,1,0:T(8,128)}, f32[10,24,128]{2,1,0:T(8,128)}, f32[10,8,128]{2,1,0:T(8,128)}, f32[264,128]{1,0:T(8,128)}) custom-call(f32[10,20,2048]{2,1,0:T(8,128)} %states.3, s32[10,2048]{1,0:T(8,128)} %flags.3), custom_call_target="tpu_custom_call" | custom-call | tf_op jit(solution)/shard_map/front/pallas_call | solution.py:406
  37.5 10.0 %inverse.1.mine = f32[264,128]{1,0:T(8,128)} custom-call(f32[264,128]{1,0:T(8,128)} %get-tuple-element.13.gram), custom_call_target="tpu_custom_call" | custom-call | tf_op jit(solution)/shard_map/inverse/pallas_call | solution.py:530
  48.2 74.9 %chain.1 = (f32[1,2048]{1,0:T(1,128)}, f32[1,128]{1,0:T(1,128)}, f32[10,231]{1,0:T(8,128)}) custom-call(f32[10,20,2048]{2,1,0:T(8,128)} %states.3, s32[10,2048]{1,0:T(8,128)} %flags.3, f32[1,2048]{1,0:T(1,128)} %bitcast.5, f32[1]{0:T(128)S(6)} %copy.12.strike, s32[1,2048]{1,0:T(1,128)} %bitcast.6, f32[10,24,128]{2,1,0:T(8,128)} %get-tuple-element.10.mean, ...), custom_call_target="tpu_custom_call" | custom-call | tf_op jit(solution)/shard_map/chain/pallas_call | solution.py:750
  123.0 1.3 %copy.13 = f32[2048]{0:T(1024)} copy(f32[2048]{0:T(1024)} %bitcast.7) | data formatting | bytes 16384
  125.0 1.3 %copy.15 = f32[10,231]{1,0:T(8,128)} copy(f32[10,231]{1,0:T(8,128)} %get-tuple-element.22) | data formatting | bytes 18480

commit v5 on v4

--- a/solution.py
+++ b/solution.py
@@ -158,7 +158,7 @@
         copy.wait_recv()
 
 
-def front_kernel(
+def front(
     states, flags, mean_out, inv_out, count_out, system_out,
     part, slots, money_of, y, parts, gram, slot_a, slot_b, sum_a, sum_b, last_a, last_b,
     send_sem, recv_sem, send_a, send_b, recv_a, recv_b,
@@ -399,49 +399,6 @@
         copy.wait_send()
 
 
-def front_call(states, flags):
-    paths = states.shape[2]
-    columns = DATES // SIDE + 1
-    dma = pltpu.SemaphoreType.DMA
-    return pl.pallas_call(
-        front_kernel,
-        name="front",
-        out_shape=(
-            jax.ShapeDtypeStruct((DATES, 24, 128), f32),
-            jax.ShapeDtypeStruct((DATES, 24, 128), f32),
-            jax.ShapeDtypeStruct((DATES, 8, 128), f32),
-            jax.ShapeDtypeStruct((PACKED, 128), f32),
-        ),
-        in_specs=[vmem()] * 2,
-        out_specs=(vmem(),) * 4,
-        scratch_shapes=[
-            pltpu.VMEM((640, 128), f32),
-            pltpu.VMEM((GROUP, 8, 128), f32),
-            pltpu.VMEM((DATES, 1, paths), f32),
-            pltpu.VMEM((24, paths), f32),
-            pltpu.VMEM((paths // 128, 768, 128), bf16),
-            pltpu.VMEM((DATES, PACKED, 128), f32),
-            pltpu.VMEM((columns, SIDE, HALF, 128), f32),
-            pltpu.VMEM((columns, SIDE, PACKED - HALF, 128), f32),
-            pltpu.VMEM((columns, HALF, 128), f32),
-            pltpu.VMEM((columns, PACKED - HALF, 128), f32),
-            pltpu.VMEM((SIDE, HALF, 128), f32),
-            pltpu.VMEM((SIDE, PACKED - HALF, 128), f32),
-            dma((GROUP,)),
-            dma((GROUP,)),
-            dma((DATES,)),
-            dma((DATES,)),
-            dma((columns, SIDE)),
-            dma((columns, SIDE)),
-            dma((columns,)),
-            dma((columns,)),
-            dma((SIDE,)),
-            dma((SIDE,)),
-        ],
-        compiler_params=pltpu.CompilerParams(collective_id=0, has_side_effects=True),
-    )(states, flags)
-
-
 def sweep_block(panel, b, start):
     height = panel.shape[0]
     columns = [
@@ -492,7 +449,7 @@
     )
 
 
-def inverse_kernel(gram, out, work):
+def invert(gram, out, work):
     rows, lanes = triangle()
     ridge = jnp.where(rows == lanes, RIDGE, 0.0).astype(f32)
     first, cross, turned, last = unpack(gram[0:128, :], gram[128:256, :], gram[256:257, :])
@@ -526,25 +483,13 @@
     out[256:264, :] = diagonal
 
 
-def inverse_call(gram):
-    return pl.pallas_call(
-        inverse_kernel,
-        name="inverse",
-        out_shape=jax.ShapeDtypeStruct((PACKED, 128), f32),
-        in_specs=[vmem()],
-        out_specs=vmem(),
-        scratch_shapes=[pltpu.VMEM((256, 256), f32)],
-    )(gram)
-
-
-def chain_kernel(
-    states, flags, terminal, strike, date_index, mean, inv, count, mine, move,
+def chain(
+    states, money_of, terminal, strike, date_index, mean, inv, count, mine, move,
     cash_out, price_out, coef_out,
     y, phi, exercise, discount, value, packed, solve, slots, slots_price, coefs,
     spread_send, spread_recv, send_sem, recv_sem, price_send, price_recv,
 ):
     me = lax.axis_index("path")
-    barrier = greet(me)
     paths = states.shape[2]
     chunks = paths // 128
 
@@ -612,8 +557,6 @@
             device_id_type=MESH_ID,
         )
 
-    fill_rest(y)
-    pl.semaphore_wait(barrier, GROUP - 1)
     own_q = lax.rem(my_z - my_x + SIDE, SIDE)
     own = own_q * SIDE + my_x
 
@@ -650,7 +593,7 @@
         par = lax.rem(t, 2)
         now = phi.at[par]
         held = value[...] * discount[par]
-        money = flags[pl.ds(d, 1), :].astype(f32)
+        money = money_of[d]
         weighted = money * held
         sums = jnp.zeros((ROWS, 128), f32)
         for c in range(chunks):
@@ -745,47 +688,103 @@
     lax.fori_loop(0, DATES, relay_done, 0)
 
 
-def chain_call(states, flags, terminal, strike, date_index, mean, inv, count, mine, move):
+FRONT_SCRATCH = 22
+
+
+def whole_kernel(states, flags, terminal, strike, date_index, move, cash, price, coefs, *scratch):
+    mean, inv, count, system, mine, work = scratch[:6]
+    front_scratch = scratch[6 : 6 + FRONT_SCRATCH]
+    money_of, y = front_scratch[2:4]
+    me = lax.axis_index("path")
+    front(states, flags, mean, inv, count, system, *front_scratch)
+    own = lax.rem(me // SIDE - lax.rem(me, SIDE) + SIDE, SIDE) * SIDE + lax.rem(me, SIDE)
+
+    @pl.when(own < DATES)
+    def _():
+        invert(system, mine, work)
+
+    chain(
+        states, money_of, terminal, strike, date_index, mean, inv, count, mine, move,
+        cash, price, coefs, y, *scratch[6 + FRONT_SCRATCH :],
+    )
+
+
+def whole_call(states, flags, terminal, strike, date_index, move):
     paths = states.shape[2]
+    columns = DATES // SIDE + 1
+    dma = pltpu.SemaphoreType.DMA
+
+    def space(*shape):
+        return pltpu.VMEM(shape, f32)
+
+    front_scratch = [
+        space(640, 128),
+        space(GROUP, 8, 128),
+        space(DATES, 1, paths),
+        space(24, paths),
+        pltpu.VMEM((paths // 128, 768, 128), bf16),
+        space(DATES, PACKED, 128),
+        space(columns, SIDE, HALF, 128),
+        space(columns, SIDE, PACKED - HALF, 128),
+        space(columns, HALF, 128),
+        space(columns, PACKED - HALF, 128),
+        space(SIDE, HALF, 128),
+        space(SIDE, PACKED - HALF, 128),
+        dma((GROUP,)),
+        dma((GROUP,)),
+        dma((DATES,)),
+        dma((DATES,)),
+        dma((columns, SIDE)),
+        dma((columns, SIDE)),
+        dma((columns,)),
+        dma((columns,)),
+        dma((SIDE,)),
+        dma((SIDE,)),
+    ]
+    assert len(front_scratch) == FRONT_SCRATCH
     return pl.pallas_call(
-        chain_kernel,
-        name="chain",
+        whole_kernel,
+        name="whole",
         out_shape=(
             jax.ShapeDtypeStruct((1, paths), f32),
             jax.ShapeDtypeStruct((1, 128), f32),
             jax.ShapeDtypeStruct((DATES, BASIS), f32),
         ),
-        in_specs=[vmem()] * 3 + [pl.BlockSpec(memory_space=pltpu.SMEM)] + [vmem()] * 6,
+        in_specs=[vmem()] * 3 + [pl.BlockSpec(memory_space=pltpu.SMEM)] + [vmem()] * 2,
         out_specs=(vmem(),) * 3,
         scratch_shapes=[
-            pltpu.VMEM((24, paths), f32),
-            pltpu.VMEM((2, ROWS, paths), f32),
-            pltpu.VMEM((2, 1, paths), f32),
-            pltpu.VMEM((2, 1, paths), f32),
-            pltpu.VMEM((1, paths), f32),
-            pltpu.VMEM((DATES, PACKED, 128), f32),
-            pltpu.VMEM((256, 256), f32),
-            pltpu.VMEM((2, GROUP, 2, 128), f32),
-            pltpu.VMEM((GROUP, 1, 128), f32),
-            pltpu.VMEM((256, 128), f32),
-            pltpu.SemaphoreType.DMA((2, 2, DATES // SIDE + 1, SIDE)),
-            pltpu.SemaphoreType.DMA((2, DATES)),
-            pltpu.SemaphoreType.DMA((2, GROUP)),
-            pltpu.SemaphoreType.DMA((2, GROUP)),
-            pltpu.SemaphoreType.DMA((GROUP,)),
-            pltpu.SemaphoreType.DMA((GROUP,)),
+            space(DATES, 24, 128),
+            space(DATES, 24, 128),
+            space(DATES, 8, 128),
+            space(PACKED, 128),
+            space(PACKED, 128),
+            space(256, 256),
+            *front_scratch,
+            space(2, ROWS, paths),
+            space(2, 1, paths),
+            space(2, 1, paths),
+            space(1, paths),
+            space(DATES, PACKED, 128),
+            space(256, 256),
+            space(2, GROUP, 2, 128),
+            space(GROUP, 1, 128),
+            space(256, 128),
+            dma((2, 2, columns, SIDE)),
+            dma((2, DATES)),
+            dma((2, GROUP)),
+            dma((2, GROUP)),
+            dma((GROUP,)),
+            dma((GROUP,)),
         ],
-        compiler_params=pltpu.CompilerParams(collective_id=2, has_side_effects=True),
-    )(states, flags, terminal, strike, date_index, mean, inv, count, mine, move)
+        compiler_params=pltpu.CompilerParams(collective_id=0, has_side_effects=True),
+    )(states, flags, terminal, strike, date_index, move)
 
 
 def shards(states, flags, terminal, strike, date_index):
     paths = states.shape[2]
-    mean, inv, count, system = front_call(states, flags)
-    packed = inverse_call(system)
-    cash, price, coefs = chain_call(
+    cash, price, coefs = whole_call(
         states, flags, terminal.reshape(1, paths), strike, date_index.reshape(1, paths),
-        mean, inv, count, packed, reference_order(),
+        reference_order(),
     )
     return cash.reshape(paths), price[0, 0:1], coefs
 

time: 128 us -> 122 us (0.953)
  Pallas kernels: 122 us -> 116 us
    pallas_call x3 -> x1, Pallas kernels: 122 us -> 116 us  [whole_call(): pl.pallas_call(whole_kernel, name='whole', out_shape=(jax.ShapeDtypeStruc...]
where the time goes in v5:
time: 122 us
  Pallas kernels  116 us (95%)
  between operations  3.05 us (2%)
  local copies, waits for them, and re-layouts  2.62 us (2%)
    pallas_call x1, Pallas kernels, whole_call(): pl.pallas_call(whole_kernel, name='whole', out_shape=(jax.ShapeDtypeStruc...  116 us
    unnamed x2, local copies, waits for them, and re-layouts  2.62 us

profile of v5, /device:TPU:0, one launch (start us, length us, event | category | flops | bytes accessed | tf_op | source)
XLA Modules:
  0.0 121.6 jit_solution(17138581099627589827)
XLA Ops:
  1.3 115.9 %whole.1 = (f32[1,2048]{1,0:T(1,128)}, f32[1,128]{1,0:T(1,128)}, f32[10,231]{1,0:T(8,128)}) custom-call(f32[10,20,2048]{2,1,0:T(8,128)} %states.1, s32[10,2048]{1,0:T(8,128)} %flags.1, f32[1,2048]{1,0:T(1,128)} %bitcast.5, f32[1]{0:T(128)S(6)} %copy.12.strike, s32[1,2048]{1,0:T(1,128)} %bitcast.6, bf16[256,256]{1,0:T(8,128)(2,1)} %constant.2.clone.move), custom_call_target="tpu_custom_call" | custom-call | tf_op jit(solution)/shard_map/whole/pallas_call | solution.py:745
  117.2 1.3 %copy.13 = f32[2048]{0:T(1024)} copy(f32[2048]{0:T(1024)} %bitcast.7) | data formatting | bytes 16384
  119.1 1.3 %copy.15 = f32[10,231]{1,0:T(8,128)} copy(f32[10,231]{1,0:T(8,128)} %get-tuple-element.14) | data formatting | bytes 18480

commit v6 on v5

--- a/solution.py
+++ b/solution.py
@@ -159,7 +159,7 @@
 
 
 def front(
-    states, flags, mean_out, inv_out, count_out, system_out,
+    meanwhile, states, flags, mean_out, inv_out, count_out, system_out,
     part, slots, money_of, y, parts, gram, slot_a, slot_b, sum_a, sum_b, last_a, last_b,
     send_sem, recv_sem, send_a, send_b, recv_a, recv_b,
     send_last_a, send_last_b, recv_last_a, recv_last_b,
@@ -344,20 +344,23 @@
             def _():
                 last_copy_b(d, k_x).start()
 
-    def date_step(d, carry):
+    def gram_step(i, carry):
+        d = DATES - 1 - i
         compute(d, parts)
         send(d)
 
-        @pl.when(d >= LAG)
-        def _():
-            collect(d - LAG)
+        @pl.when(i >= LAG)
+        def _():
+            collect(d + LAG)
 
         return carry
 
     for i in range(3):
         parts[:, 256 * i + 240 : 256 * i + 256, :] = jnp.zeros((paths // 128, 16, 128), bf16)
-    lax.fori_loop(0, DATES, date_step, 0)
-    lax.fori_loop(DATES - LAG, DATES, lambda d, carry: (collect(d), carry)[1], 0)
+    lax.fori_loop(0, DATES, gram_step, 0)
+    meanwhile()
+    for d in range(LAG - 1, -1, -1):
+        collect(d)
 
     own_q = lax.rem(my_z - my_x + SIDE, SIDE)
     own = own_q * SIDE + my_x
@@ -484,10 +487,10 @@
 
 
 def chain(
-    states, money_of, terminal, strike, date_index, mean, inv, count, mine, move,
+    middle, states, money_of, terminal, strike, date_index, mean, inv, count, mine,
     cash_out, price_out, coef_out,
-    y, phi, exercise, discount, value, packed, solve, slots, slots_price, coefs,
-    spread_send, spread_recv, send_sem, recv_sem, price_send, price_recv,
+    y, phi, exercise, discount, value, packed, solve, slots, slots_price, coefs, first_coef,
+    spread_send, spread_recv, send_sem, recv_sem, price_send, price_recv, first_send, first_recv,
 ):
     me = lax.axis_index("path")
     paths = states.shape[2]
@@ -557,10 +560,76 @@
             device_id_type=MESH_ID,
         )
 
-    own_q = lax.rem(my_z - my_x + SIDE, SIDE)
-    own = own_q * SIDE + my_x
-
-    @pl.when(own < DATES)
+    own = lax.rem(my_z - my_x + SIDE, SIDE) * SIDE + my_x
+    last = DATES - 1
+    last_owner = owner_z(last) * SIDE + owner_x(last)
+
+    def first_copy(k):
+        return pltpu.make_async_remote_copy(
+            src_ref=first_coef,
+            dst_ref=first_coef,
+            send_sem=first_send.at[k],
+            recv_sem=first_recv,
+            device_id={"path": lax.rem(me + k, GROUP)},
+            device_id_type=MESH_ID,
+        )
+
+    def send_rhs(t):
+        par = lax.rem(t, 2)
+        held = value[...] * discount[par]
+        value[...] = held
+        weighted = money_of[last - t] * held
+        sums = jnp.zeros((ROWS, 128), f32)
+        for c in range(chunks):
+            cut = slice(128 * c, 128 * c + 128)
+            sums = sums + phi[par, :, cut] * weighted[:, cut]
+        low = jnp.sum(sums[0:128, :].T, axis=0, keepdims=True)
+        high = jnp.concatenate([sums[128:ROWS, :], jnp.zeros((256 - ROWS, 128), f32)], axis=0)
+        high = jnp.sum(high.T, axis=0, keepdims=True)
+        slots[par, me] = jnp.concatenate([low, high], axis=0)
+        for k in range(1, GROUP):
+            rhs_copy(par, k).start()
+
+    def unpack_into_solve(source):
+        first, cross, turned, end = unpack(source[0:128, :], source[128:256, :], source[256:257, :])
+        solve[0:128, 0:128] = first
+        solve[0:128, 128:256] = cross
+        solve[128:256, 0:128] = turned
+        solve[128:256, 128:256] = end
+
+    def solved(t):
+        par = lax.rem(t, 2)
+        rhs = slots[par, 0]
+        for k in range(1, GROUP):
+            rhs = rhs + slots[par, k]
+        rhs = rhs / count[last - t, 0:2, :]
+        product = solve[0:ROWS, 0:128] * rhs[0:1, :] + solve[0:ROWS, 128:256] * rhs[1:2, :]
+        return jnp.broadcast_to(jnp.sum(product, axis=1, keepdims=True), (ROWS, 128))
+
+    def finish_date(t, coef):
+        d = last - t
+        par = lax.rem(t, 2)
+        lane = lax.broadcasted_iota(jnp.int32, (ROWS, 128), 1)
+        coefs[0:ROWS, :] = jnp.where(lane == d, coef, coefs[0:ROWS, :])
+        for c in range(chunks):
+            cut = slice(128 * c, 128 * c + 128)
+            continuation = jnp.sum(coef * phi[par, :, cut], axis=0, keepdims=True)
+            gain = exercise[par, :, cut]
+            open_date = (date_index[:, cut] <= d).astype(f32)
+            money = money_of[d, :, cut]
+            weight = jax.nn.sigmoid((gain - continuation) / TEMPER) * money * open_date
+            old = value[:, cut]
+            value[:, cut] = old + weight * (gain - old)
+
+    def before_collecting():
+        prepare(last, 0)
+        value[...] = terminal[...]
+        coefs[...] = jnp.zeros_like(coefs)
+        send_rhs(0)
+
+    middle(before_collecting)
+
+    @pl.when(own < last)
     def _():
         for k in range(1, SIDE):
             for half in range(2):
@@ -570,11 +639,22 @@
                 spread(mine.at[spans[half]], own, half, 1 - half, k, 1).start()
         packed[own] = mine[...]
 
-    prepare(DATES - 1, 0)
-    value[...] = terminal[...]
-    coefs[...] = jnp.zeros_like(coefs)
+    for k in range(1, GROUP):
+        rhs_copy(0, k).wait_recv()
+
+    @pl.when(me == last_owner)
+    def _():
+        unpack_into_solve(mine)
+        coef = solved(0)
+        high = jnp.concatenate([coef[128:ROWS, :], jnp.zeros((256 - ROWS, 128), f32)], axis=0)
+        first_coef[...] = jnp.concatenate([coef[0:128, :].T[0:1, :], high.T[0:1, :]], axis=0)
+        for k in range(1, GROUP):
+            first_copy(k).start()
+
+    prepare(last - 1, 1)
+
     def relay_step(t, carry):
-        d = DATES - 1 - t
+        d = last - t
         for half in range(2):
 
             @pl.when(relay(d, half) & jnp.logical_not(is_owner(d)))
@@ -586,65 +666,46 @@
 
         return carry
 
-    lax.fori_loop(0, DATES, relay_step, 0)
+    lax.fori_loop(1, DATES, relay_step, 0)
+
+    @pl.when(me != last_owner)
+    def _():
+        first_copy(1).wait_recv()
+
+    pad = jnp.zeros((127, 128), f32)
+    halves = [
+        jnp.concatenate([first_coef[i : i + 1, :], pad], axis=0).T[:, 0:1] for i in range(2)
+    ]
+    column = jnp.concatenate(halves, axis=0)[0:ROWS]
+    finish_date(0, jnp.broadcast_to(column, (ROWS, 128)))
+    for k in range(1, GROUP):
+        rhs_copy(0, k).wait_send()
+    send_rhs(1)
 
     def date_step(t, carry):
-        d = DATES - 1 - t
+        d = last - t
         par = lax.rem(t, 2)
-        now = phi.at[par]
-        held = value[...] * discount[par]
-        money = money_of[d]
-        weighted = money * held
-        sums = jnp.zeros((ROWS, 128), f32)
-        for c in range(chunks):
-            cut = slice(128 * c, 128 * c + 128)
-            sums = sums + now[0:ROWS, cut] * weighted[:, cut]
-        low = jnp.sum(sums[0:128, :].T, axis=0, keepdims=True)
-        high = jnp.concatenate([sums[128:ROWS, :], jnp.zeros((256 - ROWS, 128), f32)], axis=0)
-        high = jnp.sum(high.T, axis=0, keepdims=True)
-        slots[par, me] = jnp.concatenate([low, high], axis=0)
-        for k in range(1, GROUP):
-            rhs_copy(par, k).start()
-
         for half in range(2):
 
             @pl.when(jnp.logical_not(relay(d, half)))
             def _(half=half):
                 spread(packed.at[d, spans[half]], d, half, half, 1, 0).wait_recv()
 
-        first, cross, turned, last = unpack(
-            packed[d, 0:128, :], packed[d, 128:256, :], packed[d, 256:257, :]
-        )
-        solve[0:128, 0:128] = first
-        solve[0:128, 128:256] = cross
-        solve[128:256, 0:128] = turned
-        solve[128:256, 128:256] = last
+        unpack_into_solve(packed.at[d])
         prepare(jnp.maximum(d - 1, 0), 1 - par)
-
         for k in range(1, GROUP):
             rhs_copy(par, k).wait_recv()
-        rhs = slots[par, 0]
-        for k in range(1, GROUP):
-            rhs = rhs + slots[par, k]
-        rhs = rhs / count[d, 0:2, :]
-        product = solve[0:ROWS, 0:128] * rhs[0:1, :] + solve[0:ROWS, 128:256] * rhs[1:2, :]
-        coef = jnp.sum(product, axis=1, keepdims=True)
-        coef = jnp.broadcast_to(coef, (ROWS, 128))
-        lane = lax.broadcasted_iota(jnp.int32, (ROWS, 128), 1)
-        coefs[0:ROWS, :] = jnp.where(lane == d, coef, coefs[0:ROWS, :])
-        for c in range(chunks):
-            cut = slice(128 * c, 128 * c + 128)
-            continuation = jnp.sum(coef * now[0:ROWS, cut], axis=0, keepdims=True)
-            gain = exercise[par, :, cut]
-            open_date = (date_index[:, cut] <= d).astype(f32)
-            weight = jax.nn.sigmoid((gain - continuation) / TEMPER) * money[:, cut] * open_date
-            old = held[:, cut]
-            value[:, cut] = old + weight * (gain - old)
+        finish_date(t, solved(t))
         for k in range(1, GROUP):
             rhs_copy(par, k).wait_send()
+
+        @pl.when(t < last)
+        def _():
+            send_rhs(t + 1)
+
         return carry
 
-    lax.fori_loop(0, DATES, date_step, 0)
+    lax.fori_loop(1, DATES, date_step, 0)
 
     total = jnp.zeros((1, 128), f32)
     for c in range(chunks):
@@ -653,11 +714,9 @@
     for k in range(1, GROUP):
         price_copy(k).start()
     cash_out[...] = value[...]
-    turned = jnp.concatenate([coefs[0:128, :].T[0:16, :], coefs[128:256, :].T[0:16, :]], axis=1)
-    ordered = jnp.zeros((16, 256), f32)
-    for piece in three_parts(turned)[::-1]:
-        ordered = ordered + jnp.dot(piece, move[...], preferred_element_type=f32)
-    coef_out[...] = ordered[0:DATES, 0:BASIS]
+    coef_out[...] = jnp.concatenate(
+        [coefs[0:128, :].T[0:16, :], coefs[128:256, :].T[0:16, :]], axis=1
+    )
     for k in range(1, GROUP):
         price_copy(k).wait_recv()
     total = slots_price[0]
@@ -668,7 +727,12 @@
     for k in range(1, GROUP):
         price_copy(k).wait_send()
 
-    @pl.when(own < DATES)
+    @pl.when(me == last_owner)
+    def _():
+        for k in range(1, GROUP):
+            first_copy(k).wait_send()
+
+    @pl.when(own < last)
     def _():
         for k in range(1, SIDE):
             for half in range(2):
@@ -685,31 +749,33 @@
 
         return carry
 
-    lax.fori_loop(0, DATES, relay_done, 0)
+    lax.fori_loop(0, last, relay_done, 0)
 
 
 FRONT_SCRATCH = 22
 
 
-def whole_kernel(states, flags, terminal, strike, date_index, move, cash, price, coefs, *scratch):
+def whole_kernel(states, flags, terminal, strike, date_index, cash, price, coefs, *scratch):
     mean, inv, count, system, mine, work = scratch[:6]
     front_scratch = scratch[6 : 6 + FRONT_SCRATCH]
     money_of, y = front_scratch[2:4]
     me = lax.axis_index("path")
-    front(states, flags, mean, inv, count, system, *front_scratch)
     own = lax.rem(me // SIDE - lax.rem(me, SIDE) + SIDE, SIDE) * SIDE + lax.rem(me, SIDE)
 
-    @pl.when(own < DATES)
-    def _():
-        invert(system, mine, work)
+    def middle(meanwhile):
+        front(meanwhile, states, flags, mean, inv, count, system, *front_scratch)
+
+        @pl.when(own < DATES)
+        def _():
+            invert(system, mine, work)
 
     chain(
-        states, money_of, terminal, strike, date_index, mean, inv, count, mine, move,
+        middle, states, money_of, terminal, strike, date_index, mean, inv, count, mine,
         cash, price, coefs, y, *scratch[6 + FRONT_SCRATCH :],
     )
 
 
-def whole_call(states, flags, terminal, strike, date_index, move):
+def whole_call(states, flags, terminal, strike, date_index):
     paths = states.shape[2]
     columns = DATES // SIDE + 1
     dma = pltpu.SemaphoreType.DMA
@@ -748,9 +814,9 @@
         out_shape=(
             jax.ShapeDtypeStruct((1, paths), f32),
             jax.ShapeDtypeStruct((1, 128), f32),
-            jax.ShapeDtypeStruct((DATES, BASIS), f32),
+            jax.ShapeDtypeStruct((16, 256), f32),
         ),
-        in_specs=[vmem()] * 3 + [pl.BlockSpec(memory_space=pltpu.SMEM)] + [vmem()] * 2,
+        in_specs=[vmem()] * 3 + [pl.BlockSpec(memory_space=pltpu.SMEM)] + [vmem()],
         out_specs=(vmem(),) * 3,
         scratch_shapes=[
             space(DATES, 24, 128),
@@ -769,23 +835,49 @@
             space(2, GROUP, 2, 128),
             space(GROUP, 1, 128),
             space(256, 128),
+            space(2, 128),
             dma((2, 2, columns, SIDE)),
             dma((2, DATES)),
             dma((2, GROUP)),
             dma((2, GROUP)),
             dma((GROUP,)),
             dma((GROUP,)),
+            dma((GROUP,)),
+            dma,
         ],
         compiler_params=pltpu.CompilerParams(collective_id=0, has_side_effects=True),
-    )(states, flags, terminal, strike, date_index, move)
+    )(states, flags, terminal, strike, date_index)
+
+
+def result_kernel(cash, price, coefs, move, cash_out, price_out, coef_out):
+    cash_out[...] = cash[...]
+    price_out[...] = price[...]
+    ordered = jnp.zeros((16, 256), f32)
+    for piece in three_parts(coefs[...])[::-1]:
+        ordered = ordered + jnp.dot(piece, move[...], preferred_element_type=f32)
+    coef_out[...] = ordered[0:DATES, 0:BASIS]
+
+
+def result_call(cash, price, coefs):
+    return pl.pallas_call(
+        result_kernel,
+        name="result",
+        out_shape=(
+            jax.ShapeDtypeStruct(cash.shape, f32),
+            jax.ShapeDtypeStruct((1, 128), f32),
+            jax.ShapeDtypeStruct((DATES, BASIS), f32),
+        ),
+        in_specs=[vmem()] * 4,
+        out_specs=(vmem(),) * 3,
+    )(cash, price, coefs, reference_order())
 
 
 def shards(states, flags, terminal, strike, date_index):
     paths = states.shape[2]
-    cash, price, coefs = whole_call(
-        states, flags, terminal.reshape(1, paths), strike, date_index.reshape(1, paths),
-        reference_order(),
+    whole = whole_call(
+        states, flags, terminal.reshape(1, paths), strike, date_index.reshape(1, paths)
     )
+    cash, price, coefs = result_call(*whole)
     return cash.reshape(paths), price[0, 0:1], coefs
 
 

time: 122 us -> 113 us (0.926)
  Pallas kernels: 116 us -> 112 us
  local copies, waits for them, and re-layouts: 2.62 us -> 0 us
  between operations: 3.05 us -> 1.29 us
    pallas_call x1, Pallas kernels: 116 us -> 110 us  [whole_call(): pl.pallas_call(whole_kernel, name='whole', out_shape=(jax.ShapeDtypeStruc...]
    unnamed x2 -> x0, local copies, waits for them, and re-layouts: 2.62 us -> none
    pallas_call x0 -> x1, Pallas kernels: none -> 1.74 us  [result_call(): pl.pallas_call(result_kernel, name='result', out_shape=(jax.ShapeDtypeStr...]
where the time goes in v6:
time: 113 us
  Pallas kernels  112 us (99%)
  between operations  1.29 us (1%)
    pallas_call x1, Pallas kernels, whole_call(): pl.pallas_call(whole_kernel, name='whole', out_shape=(jax.ShapeDtypeStruc...  110 us

profile of v6, /device:TPU:0, one launch (start us, length us, event | category | flops | bytes accessed | tf_op | source)
XLA Modules:
  0.0 113.2 jit_solution(3876042866945083061)
XLA Ops:
  1.3 110.2 %whole.1 = (f32[1,2048]{1,0:T(1,128)}, f32[1,128]{1,0:T(1,128)}, f32[16,256]{1,0:T(8,128)}) custom-call(f32[10,20,2048]{2,1,0:T(8,128)} %states.1, s32[10,2048]{1,0:T(8,128)} %flags.1, f32[1,2048]{1,0:T(1,128)} %bitcast.5, f32[1]{0:T(128)S(6)} %copy.9.strike, s32[1,2048]{1,0:T(1,128)} %bitcast.6), custom_call_target="tpu_custom_call" | custom-call | tf_op jit(solution)/shard_map/whole/pallas_call | solution.py:811
  111.5 1.7 %result.1 = (f32[1,2048]{1,0:T(1,128)}, f32[1,128]{1,0:T(1,128)}, f32[10,231]{1,0:T(8,128)}) custom-call(f32[1,2048]{1,0:T(1,128)} %get-tuple-element.9.cash, f32[1,128]{1,0:T(1,128)} %get-tuple-element.10.price, f32[16,256]{1,0:T(8,128)} %get-tuple-element.11.coefs, bf16[256,256]{1,0:T(8,128)(2,1)} %constant.2.clone.move), custom_call_target="tpu_custom_call" | custom-call | tf_op jit(solution)/shard_map/result/pallas_call | solution.py:862

commit v7 on v6

--- a/solution.py
+++ b/solution.py
@@ -21,9 +21,10 @@
 PACKED = 264
 HALF = 136
 SIDE = 4
-LAG = 2
+LAG = 4
 CHUNKS = 8
 MESH_ID = pl.DeviceIdType.MESH
+FAR_FIRST = sorted(range(1, GROUP), key=lambda k: -(min(k // 4, 4 - k // 4) + min(k % 4, 4 - k % 4)))
 
 
 def basis_pairs():
@@ -452,7 +453,7 @@
     )
 
 
-def invert(gram, out, work):
+def invert(packing, gram, out, work):
     rows, lanes = triangle()
     ridge = jnp.where(rows == lanes, RIDGE, 0.0).astype(f32)
     first, cross, turned, last = unpack(gram[0:128, :], gram[128:256, :], gram[256:257, :])
@@ -480,14 +481,17 @@
             current = jnp.where(kept[0:32, :], work[after : after + 32, :], 0.0) - change
         work[...] = jnp.where(kept, work[...], 0.0) - transposed_product(left, right)
         work[top : top + deep, :] = panel[0:deep, :]
-    mixed, diagonal = pack(-work[0:128, 0:128], -work[128:256, 128:256])
-    out[0:128, :] = -work[0:128, 128:256]
-    out[128:256, :] = mixed
-    out[256:264, :] = diagonal
+
+    @pl.when(packing)
+    def _():
+        mixed, diagonal = pack(-work[0:128, 0:128], -work[128:256, 128:256])
+        out[0:128, :] = -work[0:128, 128:256]
+        out[128:256, :] = mixed
+        out[256:264, :] = diagonal
 
 
 def chain(
-    middle, states, money_of, terminal, strike, date_index, mean, inv, count, mine,
+    middle, states, money_of, terminal, strike, date_index, mean, inv, count, mine, work,
     cash_out, price_out, coef_out,
     y, phi, exercise, discount, value, packed, solve, slots, slots_price, coefs, first_coef,
     spread_send, spread_recv, send_sem, recv_sem, price_send, price_recv, first_send, first_recv,
@@ -587,7 +591,7 @@
         high = jnp.concatenate([sums[128:ROWS, :], jnp.zeros((256 - ROWS, 128), f32)], axis=0)
         high = jnp.sum(high.T, axis=0, keepdims=True)
         slots[par, me] = jnp.concatenate([low, high], axis=0)
-        for k in range(1, GROUP):
+        for k in FAR_FIRST:
             rhs_copy(par, k).start()
 
     def unpack_into_solve(source):
@@ -644,11 +648,11 @@
 
     @pl.when(me == last_owner)
     def _():
-        unpack_into_solve(mine)
+        solve[...] = -work[...]
         coef = solved(0)
         high = jnp.concatenate([coef[128:ROWS, :], jnp.zeros((256 - ROWS, 128), f32)], axis=0)
         first_coef[...] = jnp.concatenate([coef[0:128, :].T[0:1, :], high.T[0:1, :]], axis=0)
-        for k in range(1, GROUP):
+        for k in FAR_FIRST:
             first_copy(k).start()
 
     prepare(last - 1, 1)
@@ -678,8 +682,6 @@
     ]
     column = jnp.concatenate(halves, axis=0)[0:ROWS]
     finish_date(0, jnp.broadcast_to(column, (ROWS, 128)))
-    for k in range(1, GROUP):
-        rhs_copy(0, k).wait_send()
     send_rhs(1)
 
     def date_step(t, carry):
@@ -694,10 +696,10 @@
         unpack_into_solve(packed.at[d])
         prepare(jnp.maximum(d - 1, 0), 1 - par)
         for k in range(1, GROUP):
+            rhs_copy(1 - par, k).wait_send()
+        for k in range(1, GROUP):
             rhs_copy(par, k).wait_recv()
         finish_date(t, solved(t))
-        for k in range(1, GROUP):
-            rhs_copy(par, k).wait_send()
 
         @pl.when(t < last)
         def _():
@@ -711,7 +713,7 @@
     for c in range(chunks):
         total = total + value[:, 128 * c : 128 * c + 128]
     slots_price[me] = total
-    for k in range(1, GROUP):
+    for k in FAR_FIRST:
         price_copy(k).start()
     cash_out[...] = value[...]
     coef_out[...] = jnp.concatenate(
@@ -726,6 +728,7 @@
     price_out[...] = jnp.broadcast_to(price, (1, 128))
     for k in range(1, GROUP):
         price_copy(k).wait_send()
+        rhs_copy(last % 2, k).wait_send()
 
     @pl.when(me == last_owner)
     def _():
@@ -767,10 +770,10 @@
 
         @pl.when(own < DATES)
         def _():
-            invert(system, mine, work)
+            invert(own != DATES - 1, system, mine, work)
 
     chain(
-        middle, states, money_of, terminal, strike, date_index, mean, inv, count, mine,
+        middle, states, money_of, terminal, strike, date_index, mean, inv, count, mine, work,
         cash, price, coefs, y, *scratch[6 + FRONT_SCRATCH :],
     )
 

time: 113 us -> 111 us (0.982)
  Pallas kernels: 112 us -> 110 us
    pallas_call x1, Pallas kernels: 110 us -> 108 us  [whole_call(): pl.pallas_call(whole_kernel, name='whole', out_shape=(jax.ShapeDtypeStruc...]
where the time goes in v7:
time: 111 us
  Pallas kernels  110 us (99%)
  between operations  1.29 us (1%)
    pallas_call x1, Pallas kernels, whole_call(): pl.pallas_call(whole_kernel, name='whole', out_shape=(jax.ShapeDtypeStruc...  108 us

profile of v7, /device:TPU:0, one launch (start us, length us, event | category | flops | bytes accessed | tf_op | source)
XLA Modules:
  0.0 110.9 jit_solution(4245533429352956038)
XLA Ops:
  1.3 107.8 %whole.1 = (f32[1,2048]{1,0:T(1,128)}, f32[1,128]{1,0:T(1,128)}, f32[16,256]{1,0:T(8,128)}) custom-call(f32[10,20,2048]{2,1,0:T(8,128)} %states.1, s32[10,2048]{1,0:T(8,128)} %flags.1, f32[1,2048]{1,0:T(1,128)} %bitcast.5, f32[1]{0:T(128)S(6)} %copy.9.strike, s32[1,2048]{1,0:T(1,128)} %bitcast.6), custom_call_target="tpu_custom_call" | custom-call | tf_op jit(solution)/shard_map/whole/pallas_call | solution.py:814
  109.1 1.7 %result.1 = (f32[1,2048]{1,0:T(1,128)}, f32[1,128]{1,0:T(1,128)}, f32[10,231]{1,0:T(8,128)}) custom-call(f32[1,2048]{1,0:T(1,128)} %get-tuple-element.9.cash, f32[1,128]{1,0:T(1,128)} %get-tuple-element.10.price, f32[16,256]{1,0:T(8,128)} %get-tuple-element.11.coefs, bf16[256,256]{1,0:T(8,128)(2,1)} %constant.2.clone.move), custom_call_target="tpu_custom_call" | custom-call | tf_op jit(solution)/shard_map/result/pallas_call | solution.py:865

commit v8 on v7

--- a/solution.py
+++ b/solution.py
@@ -22,6 +22,7 @@
 HALF = 136
 SIDE = 4
 LAG = 4
+AHEAD = 3
 CHUNKS = 8
 MESH_ID = pl.DeviceIdType.MESH
 FAR_FIRST = sorted(range(1, GROUP), key=lambda k: -(min(k // 4, 4 - k // 4) + min(k % 4, 4 - k % 4)))
@@ -491,7 +492,7 @@
 
 
 def chain(
-    middle, states, money_of, terminal, strike, date_index, mean, inv, count, mine, work,
+    middle, states, money_of, terminal, strike, date_index, mean, inv, count, mine, work, move,
     cash_out, price_out, coef_out,
     y, phi, exercise, discount, value, packed, solve, slots, slots_price, coefs, first_coef,
     spread_send, spread_recv, send_sem, recv_sem, price_send, price_recv, first_send, first_recv,
@@ -638,9 +639,6 @@
         for k in range(1, SIDE):
             for half in range(2):
                 spread(mine.at[spans[half]], own, half, half, k, 0).start()
-        for k in range(1, SIDE):
-            for half in range(2):
-                spread(mine.at[spans[half]], own, half, 1 - half, k, 1).start()
         packed[own] = mine[...]
 
     for k in range(1, GROUP):
@@ -657,20 +655,22 @@
 
     prepare(last - 1, 1)
 
-    def relay_step(t, carry):
-        d = last - t
+    def relay_date(d):
         for half in range(2):
 
-            @pl.when(relay(d, half) & jnp.logical_not(is_owner(d)))
+            @pl.when(relay(d, half))
             def _(half=half):
                 source = packed.at[d, spans[half]]
-                spread(source, d, half, half, 1, 0).wait_recv()
+
+                @pl.when(jnp.logical_not(is_owner(d)))
+                def _():
+                    spread(source, d, half, half, 1, 0).wait_recv()
+
                 for k in range(1, SIDE):
                     spread(source, d, half, 1 - half, k, 1).start()
 
-        return carry
-
-    lax.fori_loop(1, DATES, relay_step, 0)
+    for t in range(1, AHEAD):
+        relay_date(last - t)
 
     @pl.when(me != last_owner)
     def _():
@@ -693,6 +693,11 @@
             def _(half=half):
                 spread(packed.at[d, spans[half]], d, half, half, 1, 0).wait_recv()
 
+
+        @pl.when(t + AHEAD <= last + 1)
+        def _():
+            relay_date(last + 1 - t - AHEAD)
+
         unpack_into_solve(packed.at[d])
         prepare(jnp.maximum(d - 1, 0), 1 - par)
         for k in range(1, GROUP):
@@ -716,9 +721,11 @@
     for k in FAR_FIRST:
         price_copy(k).start()
     cash_out[...] = value[...]
-    coef_out[...] = jnp.concatenate(
-        [coefs[0:128, :].T[0:16, :], coefs[128:256, :].T[0:16, :]], axis=1
-    )
+    turned = jnp.concatenate([coefs[0:128, :].T[0:16, :], coefs[128:256, :].T[0:16, :]], axis=1)
+    ordered = jnp.zeros((16, 256), f32)
+    for piece in three_parts(turned)[::-1]:
+        ordered = ordered + jnp.dot(piece, move[...], preferred_element_type=f32)
+    coef_out[...] = ordered[0:DATES, 0:BASIS]
     for k in range(1, GROUP):
         price_copy(k).wait_recv()
     total = slots_price[0]
@@ -740,12 +747,11 @@
         for k in range(1, SIDE):
             for half in range(2):
                 spread(mine.at[spans[half]], own, half, half, k, 0).wait_send()
-                spread(mine.at[spans[half]], own, half, 1 - half, k, 1).wait_send()
 
     def relay_done(d, carry):
         for half in range(2):
 
-            @pl.when(relay(d, half) & jnp.logical_not(is_owner(d)))
+            @pl.when(relay(d, half))
             def _(half=half):
                 for k in range(1, SIDE):
                     spread(packed.at[d, spans[half]], d, half, 1 - half, k, 1).wait_send()
@@ -758,7 +764,7 @@
 FRONT_SCRATCH = 22
 
 
-def whole_kernel(states, flags, terminal, strike, date_index, cash, price, coefs, *scratch):
+def whole_kernel(states, flags, terminal, strike, date_index, move, cash, price, coefs, *scratch):
     mean, inv, count, system, mine, work = scratch[:6]
     front_scratch = scratch[6 : 6 + FRONT_SCRATCH]
     money_of, y = front_scratch[2:4]
@@ -773,12 +779,12 @@
             invert(own != DATES - 1, system, mine, work)
 
     chain(
-        middle, states, money_of, terminal, strike, date_index, mean, inv, count, mine, work,
+        middle, states, money_of, terminal, strike, date_index, mean, inv, count, mine, work, move,
         cash, price, coefs, y, *scratch[6 + FRONT_SCRATCH :],
     )
 
 
-def whole_call(states, flags, terminal, strike, date_index):
+def whole_call(states, flags, terminal, strike, date_index, move):
     paths = states.shape[2]
     columns = DATES // SIDE + 1
     dma = pltpu.SemaphoreType.DMA
@@ -817,9 +823,9 @@
         out_shape=(
             jax.ShapeDtypeStruct((1, paths), f32),
             jax.ShapeDtypeStruct((1, 128), f32),
-            jax.ShapeDtypeStruct((16, 256), f32),
+            jax.ShapeDtypeStruct((DATES, BASIS), f32),
         ),
-        in_specs=[vmem()] * 3 + [pl.BlockSpec(memory_space=pltpu.SMEM)] + [vmem()],
+        in_specs=[vmem()] * 3 + [pl.BlockSpec(memory_space=pltpu.SMEM)] + [vmem()] * 2,
         out_specs=(vmem(),) * 3,
         scratch_shapes=[
             space(DATES, 24, 128),
@@ -849,36 +855,30 @@
             dma,
         ],
         compiler_params=pltpu.CompilerParams(collective_id=0, has_side_effects=True),
-    )(states, flags, terminal, strike, date_index)
-
-
-def result_kernel(cash, price, coefs, move, cash_out, price_out, coef_out):
+    )(states, flags, terminal, strike, date_index, move)
+
+
+def result_kernel(cash, price, coefs, cash_out, price_out, coef_out):
     cash_out[...] = cash[...]
     price_out[...] = price[...]
-    ordered = jnp.zeros((16, 256), f32)
-    for piece in three_parts(coefs[...])[::-1]:
-        ordered = ordered + jnp.dot(piece, move[...], preferred_element_type=f32)
-    coef_out[...] = ordered[0:DATES, 0:BASIS]
+    coef_out[...] = coefs[...]
 
 
 def result_call(cash, price, coefs):
     return pl.pallas_call(
         result_kernel,
         name="result",
-        out_shape=(
-            jax.ShapeDtypeStruct(cash.shape, f32),
-            jax.ShapeDtypeStruct((1, 128), f32),
-            jax.ShapeDtypeStruct((DATES, BASIS), f32),
-        ),
-        in_specs=[vmem()] * 4,
+        out_shape=tuple(jax.ShapeDtypeStruct(a.shape, f32) for a in (cash, price, coefs)),
+        in_specs=[vmem()] * 3,
         out_specs=(vmem(),) * 3,
-    )(cash, price, coefs, reference_order())
+    )(cash, price, coefs)
 
 
 def shards(states, flags, terminal, strike, date_index):
     paths = states.shape[2]
     whole = whole_call(
-        states, flags, terminal.reshape(1, paths), strike, date_index.reshape(1, paths)
+        states, flags, terminal.reshape(1, paths), strike, date_index.reshape(1, paths),
+        reference_order(),
     )
     cash, price, coefs = result_call(*whole)
     return cash.reshape(paths), price[0, 0:1], coefs

time: 111 us -> 105 us (0.946)
  Pallas kernels: 110 us -> 104 us
    pallas_call x1, Pallas kernels: 108 us -> 102 us  [whole_call(): pl.pallas_call(whole_kernel, name='whole', out_shape=(jax.ShapeDtypeStruc...]
where the time goes in v8:
time: 105 us
  Pallas kernels  104 us (99%)
  between operations  1.29 us (1%)
    pallas_call x1, Pallas kernels, whole_call(): pl.pallas_call(whole_kernel, name='whole', out_shape=(jax.ShapeDtypeStruc...  102 us

profile of v8, /device:TPU:0, one launch (start us, length us, event | category | flops | bytes accessed | tf_op | source)
XLA Modules:
  0.0 104.9 jit_solution(16242992755313733935)
XLA Ops:
  1.3 102.3 %whole.1 = (f32[1,2048]{1,0:T(1,128)}, f32[1,128]{1,0:T(1,128)}, f32[10,231]{1,0:T(8,128)}) custom-call(f32[10,20,2048]{2,1,0:T(8,128)} %states.1, s32[10,2048]{1,0:T(8,128)} %flags.1, f32[1,2048]{1,0:T(1,128)} %bitcast.5, f32[1]{0:T(128)S(6)} %copy.9.strike, s32[1,2048]{1,0:T(1,128)} %bitcast.6, bf16[256,256]{1,0:T(8,128)(2,1)} %constant.2.clone.move), custom_call_target="tpu_custom_call" | custom-call | tf_op jit(solution)/shard_map/whole/pallas_call | solution.py:820
  103.6 1.4 %result.1 = (f32[1,2048]{1,0:T(1,128)}, f32[1,128]{1,0:T(1,128)}, f32[10,231]{1,0:T(8,128)}) custom-call(f32[1,2048]{1,0:T(1,128)} %get-tuple-element.9.cash, f32[1,128]{1,0:T(1,128)} %get-tuple-element.10.price, f32[10,231]{1,0:T(8,128)} %get-tuple-element.11.coefs), custom_call_target="tpu_custom_call" | custom-call | tf_op jit(solution)/shard_map/result/pallas_call | solution.py:868

commit v9 on v8

--- a/solution.py
+++ b/solution.py
@@ -21,7 +21,7 @@
 PACKED = 264
 HALF = 136
 SIDE = 4
-LAG = 4
+LAG = 3
 AHEAD = 3
 CHUNKS = 8
 MESH_ID = pl.DeviceIdType.MESH

time: 105 us -> 105 us (level)
  no operation moved by 1% of the time
where the time goes in v9:
time: 105 us
  Pallas kernels  103 us (98%)
  between operations  1.29 us (1%)
    pallas_call x1, Pallas kernels, whole_call(): pl.pallas_call(whole_kernel, name='whole', out_shape=(jax.ShapeDtypeStruc...  102 us

profile of v9, /device:TPU:0, one launch (start us, length us, event | category | flops | bytes accessed | tf_op | source)
XLA Modules:
  0.0 104.8 jit_solution(14271491936832458313)
XLA Ops:
  1.3 102.1 %whole.1 = (f32[1,2048]{1,0:T(1,128)}, f32[1,128]{1,0:T(1,128)}, f32[10,231]{1,0:T(8,128)}) custom-call(f32[10,20,2048]{2,1,0:T(8,128)} %states.1, s32[10,2048]{1,0:T(8,128)} %flags.1, f32[1,2048]{1,0:T(1,128)} %bitcast.5, f32[1]{0:T(128)S(6)} %copy.9.strike, s32[1,2048]{1,0:T(1,128)} %bitcast.6, bf16[256,256]{1,0:T(8,128)(2,1)} %constant.2.clone.move), custom_call_target="tpu_custom_call" | custom-call | tf_op jit(solution)/shard_map/whole/pallas_call | solution.py:820
  103.4 1.4 %result.1 = (f32[1,2048]{1,0:T(1,128)}, f32[1,128]{1,0:T(1,128)}, f32[10,231]{1,0:T(8,128)}) custom-call(f32[1,2048]{1,0:T(1,128)} %get-tuple-element.9.cash, f32[1,128]{1,0:T(1,128)} %get-tuple-element.10.price, f32[10,231]{1,0:T(8,128)} %get-tuple-element.11.coefs), custom_call_target="tpu_custom_call" | custom-call | tf_op jit(solution)/shard_map/result/pallas_call | solution.py:868
